TPU v7x, 512 devices: a whole 4x4x16 slice. The times are simulated.
512 devices in a mesh: obs: 16 (over x, y), patch: 32 (over z, core).
Axes of the slice: x: 4, y: 4, z: 16, core: 2. Of those that a mesh axis runs over, the one named last changes fastest.
Arguments:
- green: float32 [20480, 20480], P('obs', 'patch'), may hold values from -0.0390625 to 0.0390625
- data: float32 [20480, 128], P('obs'), may hold values from -6 to 6
- neighbours: int32 [3, 20480], P(None, 'patch'), may hold values from 0 to 20479, as said below
- reg_weight: float32 [128], replicated, may hold values from 0.5 to 2
Outputs:
- slip: float32 [20480, 128], P('patch')
Inputs may be any that keep to these rules, and one draw needn't show every extreme that they name: `neighbours`: entry (k, i) is a patch within 128 of i; an entry equal to i is padding. Distance 128 is reached in every draw.
All inputs are finite; a program needn't handle non-finite values.
Results may differ from a plain program's by a relative error of at most 0.0001.
Values sent between devices are 32-bit elements; how exact they have to be, the bound alone decides.
A program may use at most 64 MiB of HBM per device.

v0:
```python
import functools
import math

import jax
import jax.numpy as jnp
from jax import lax
from jax.experimental import pallas as pl
from jax.experimental.pallas import tpu as pltpu
from jax.sharding import PartitionSpec as P

BAND = 128
ITERS = 3
MESH = pl.DeviceIdType.MESH
F32 = jnp.float32
BF16 = jnp.bfloat16


def dot(a, b):
    return lax.dot_general(a, b, (((1,), (0,)), ((), ())), preferred_element_type=F32)


def split(x):
    hi = x.astype(BF16)
    return hi, (x - hi.astype(F32)).astype(BF16)


def kernel(n_obs, n_patch, nc, bc, green, data, nb, rw, out,
           ghi, glo, gthi, gtlo, lm, lmt, cat_d, cat_r, cat_e,
           d, g, a, wext, slip, sq, hd, hg, qd, qg,
           pf, s, rd, sr, sl, rl, rr, img, bb, br, hal, wr, scs, scr, pls, plr,
           sem_d, sem_l, sem_r, sem_i, sem_b, sem_h, sem_w, sem_s, sem_p, sem_n):
    rows, cols = green.shape
    E = data.shape[1]
    R = rows // 2 // nc
    BR = cols // bc
    half = rows // 2
    per = 4
    lag = 4
    CB = cols // BAND
    nz = n_patch // 2
    nbit = n_obs.bit_length() - 1
    obs = lax.axis_index("obs")
    pat = lax.axis_index("patch")
    z = pat // 2
    c = pat % 2
    other = 1 - c
    partner = z * 2 + other
    has_l, has_r = pat > 0, pat < n_patch - 1
    up, down = z < nz - 1, z > 0
    weight = rw[...]

    def at(o, q):
        return (o, q)

    def rcopy(src, dst, sems, dev):
        return pltpu.make_async_remote_copy(
            src_ref=src, dst_ref=dst, send_sem=sems[0], recv_sem=sems[1],
            device_id=dev, device_id_type=MESH)

    def pair(sem, *idx):
        return sem.at[(0,) + idx], sem.at[(1,) + idx]

    barrier = pltpu.get_barrier_semaphore()

    @pl.loop(1, n_patch)
    def _(i):
        pl.semaphore_signal(barrier, inc=1, device_id=at(obs, (pat + i) % n_patch), device_id_type=MESH)

    n_plane = 2 * n_obs

    def plane(i):
        q = (obs * 2 + c + i) % n_plane
        return q // 2, z * 2 + q % 2

    @pl.loop(1, n_plane)
    def _(i):
        pl.semaphore_signal(barrier, inc=1, device_id=plane(i), device_id_type=MESH)

    nblk = rows // BAND

    @pl.loop(0, nblk)
    def _(i):
        r0 = pl.multiple_of(i * BAND, BAND)
        block = green[pl.ds(r0, BAND), :]
        hi, lo = split(block)
        ghi[pl.ds(r0, BAND), :] = hi
        glo[pl.ds(r0, BAND), :] = lo
        hi, lo = split(block.T)
        gthi[:, pl.ds(r0, BAND)] = hi
        gtlo[:, pl.ds(r0, BAND)] = lo
        hi, lo = split(data[pl.ds(r0, BAND), :])
        cat_r[pl.ds(r0, BAND), 0:E] = hi
        cat_r[pl.ds(r0, BAND), E:2 * E] = lo

    scs[...] = jnp.zeros((ITERS, 8, E), F32)
    zero_c = jnp.zeros((nc, R, E), F32)
    zero_h = jnp.zeros((BAND, E), F32)

    @pl.when(z == 0)
    def _():
        for it in range(ITERS):
            rl[it] = zero_c

    @pl.when(z == nz - 1)
    def _():
        for it in range(ITERS):
            rr[it] = zero_c

    @pl.when(pat == 0)
    def _():
        for it in range(ITERS):
            hal[it, 0] = zero_h
        for it in range(ITERS - 1):
            wr[it, 0] = zero_h

    @pl.when(pat == n_patch - 1)
    def _():
        for it in range(ITERS):
            hal[it, 1] = zero_h
        for it in range(ITERS - 1):
            wr[it, 1] = zero_h

    def build_laplace():
        @pl.loop(0, CB + 2)
        def _(j):
            r0 = pl.multiple_of(j * BAND, BAND)
            col = lax.broadcasted_iota(jnp.int32, (BAND, cols), 0) + j * BAND
            own = lax.broadcasted_iota(jnp.int32, (BAND, cols), 1) + BAND
            m = jnp.where(col == own, 4.0, 0.0)
            col = col + (pat * cols - BAND)
            for k in range(3):
                m = m - jnp.where(col == nb[k:k + 1, :], 1.0, 0.0)
            lmt[pl.ds(r0, BAND), :] = m.astype(BF16)
            lm[:, pl.ds(r0, BAND)] = m.T.astype(BF16)

    pl.semaphore_wait(barrier, n_patch - 1 + n_plane - 1)

    def bit_partner(p, j):
        b0, b1 = 1 << p, 1 << (nbit - 1 - p)
        bit = b0 + (j % 2) * (b1 - b0)
        return at(obs + bit * (1 - 2 * ((obs // bit) % 2)), pat)

    def bcopy(b, p, j):
        return rcopy(bb.at[b, p, j], br.at[b, p, j], pair(sem_b, b, p, j), bit_partner(p, j))

    def backward(b, hook, dst):
        for m in range(0, bc, per):
            y = dot(gthi[m * BR:(m + per) * BR, :], cat_r[...])
            y = y[:, :E] + y[:, E:] + dot(gtlo[m * BR:(m + per) * BR, :], cat_r[:, 0:E])
            bb[b, 0, m:m + per] = y.reshape(per, BR, E)
            for j in range(m, m + per):
                bcopy(b, 0, j).start()

        hook()
        for p in range(1, nbit):
            @pl.loop(0, bc)
            def _(j):
                bcopy(b, p - 1, j).wait_recv()
                bb[b, p, j] = bb[b, p - 1, j] + br[b, p - 1, j]
                bcopy(b, p, j).start()

        @pl.loop(0, bc)
        def _(j):
            bcopy(b, nbit - 1, j).wait_recv()
            dst[pl.ds(pl.multiple_of(j * BR, BR), BR), :] = bb[b, nbit - 1, j] + br[b, nbit - 1, j]

        for p in range(nbit):
            @pl.loop(0, bc)
            def _(j):
                bcopy(b, p, j).wait_send()

    def dcopy(it, k):
        return rcopy(pf.at[k], rd.at[it, k], pair(sem_d, it, k), at(obs, partner))

    def rcopy_up(it, src, k):
        return rcopy(src.at[k], rl.at[it, k], pair(sem_l, it, k), at(obs, pat + 2))

    def rcopy_down(it, src, k):
        return rcopy(src.at[k], rr.at[it, k], pair(sem_r, it, k), at(obs, pat - 2))

    def icopy(it, k):
        return rcopy(img.at[it, c, k], img.at[it, c, k], pair(sem_i, it, k), at(obs, partner))

    def put_cat(h, k, value):
        hi, lo = split(value)
        r0 = pl.multiple_of((h * nc + k) * R, R)
        cat_r[pl.ds(r0, R), 0:E] = hi
        cat_r[pl.ds(r0, R), E:2 * E] = lo

    def hcopy_r(it):
        return rcopy((a if it else g).at[pl.ds(cols - BAND, BAND)], hal.at[it, 0], pair(sem_h, it, 0), at(obs, pat + 1))

    def hcopy_l(it):
        return rcopy((a if it else g).at[pl.ds(0, BAND)], hal.at[it, 1], pair(sem_h, it, 1), at(obs, pat - 1))

    def forward(it, sums, hook):
        last = it == ITERS - 1

        @pl.when(has_r)
        def _():
            hcopy_r(it).start()

        @pl.when(has_l)
        def _():
            hcopy_l(it).start()

        hi, lo = split((a if it else g)[...])
        cat_d[:, 0:E] = hi
        cat_d[:, E:2 * E] = lo
        sums()

        def part(h):
            r0 = pl.multiple_of(h * half, half)
            y = dot(ghi[pl.ds(r0, half), :], cat_d[...])
            y = y[:, :E] + y[:, E:] + dot(glo[pl.ds(r0, half), :], cat_d[:, 0:E])
            return y.reshape(nc, R, E)

        pf[...] = part(other)

        @pl.loop(0, nc)
        def _(k):
            dcopy(it, k).start()

        s[...] = part(c)

        @pl.loop(0, nc)
        def _(k):
            dcopy(it, k).wait_recv()
            s[k] += rd[it, k]

            @pl.when(z == 0)
            def _():
                rcopy_up(it, s, k).start()

            @pl.when(z == nz - 1)
            def _():
                rcopy_down(it, s, k).start()

        def chain(t, ends=True):
            kl = t - lag * z
            kr = t - lag * (nz - 1 - z)
            kt = t - lag * jnp.maximum(z, nz - 1 - z)

            @pl.when(down & (kl >= 0) & (kl < nc))
            def _():
                rcopy_up(it, sr, kl).wait_recv()

                @pl.when(up)
                def _():
                    sr[kl] = rl[it, kl] + s[kl]
                    rcopy_up(it, sr, kl).start()

            @pl.when(up & (kr >= 0) & (kr < nc))
            def _():
                rcopy_down(it, sl, kr).wait_recv()

                @pl.when(down)
                def _():
                    sl[kr] = rr[it, kr] + s[kr]
                    rcopy_down(it, sl, kr).start()

            if not ends:
                return

            @pl.when((kt >= 0) & (kt < nc))
            def _():
                total = rl[it, kt] + s[kt] + rr[it, kt]
                if it:
                    step, ratio = scalars
                    rest = qg[kt] - step * total
                    total = rest + ratio * qd[kt]
                if not last:
                    qg[kt] = rest if it else total
                    qd[kt] = total
                if last:
                    sq[...] += jnp.sum((total * total).reshape(R // 8, 8, E), axis=0)
                else:
                    img[it, c, kt] = total
                    icopy(it, kt).start()
                    put_cat(c, kt, total)

        if last:
            sq[...] = jnp.zeros((8, E), F32)
        pl.loop(lag, lag * (nz // 2))(functools.partial(chain, ends=False))
        scalars = hook()
        pl.loop(lag * (nz // 2), nc + lag * (nz - 1))(chain)

        if not last:
            @pl.loop(0, nc)
            def _(k):
                icopy(it, k).wait_recv()
                put_cat(other, k, img[it, other, k])

        @pl.loop(0, nc)
        def _(k):
            dcopy(it, k).wait_send()
            if not last:
                icopy(it, k).wait_send()

            @pl.when(up)
            def _():
                rcopy_up(it, sr, k).wait_send()

            @pl.when(down)
            def _():
                rcopy_down(it, sl, k).wait_send()

    def halo_wait(it):
        @pl.when(has_l)
        def _():
            hcopy_r(it).wait_recv()

        @pl.when(has_r)
        def _():
            hcopy_l(it).wait_recv()

        @pl.when(has_r)
        def _():
            hcopy_r(it).wait_send()

        @pl.when(has_l)
        def _():
            hcopy_l(it).wait_send()

    def laplace():
        for r0, n, v in ((0, BAND, hd[0]), (BAND, cols, d[...]), (BAND + cols, BAND, hd[1])):
            hi, lo = split(v)
            cat_e[r0:r0 + n, 0:E] = hi
            cat_e[r0:r0 + n, E:2 * E] = lo

    def lap_rows(i):
        r0 = pl.multiple_of(i * BAND, BAND)
        y = dot(lm[pl.ds(r0, BAND), :], cat_e[...])
        return r0, weight * (y[:, :E] + y[:, E:])

    def wcopy_l(it):
        return rcopy(wext.at[pl.ds(0, BAND)], wr.at[it, 1], pair(sem_w, it, 1), at(obs, pat - 1))

    def wcopy_r(it):
        return rcopy(wext.at[pl.ds(BAND + cols, BAND)], wr.at[it, 0], pair(sem_w, it, 0), at(obs, pat + 1))

    def reg_start(it):
        laplace()

        @pl.loop(0, CB)
        def _(i):
            r0, u = lap_rows(i)
            hi, lo = split(u)
            cat_d[pl.ds(r0, BAND), 0:E] = hi
            cat_d[pl.ds(r0, BAND), E:2 * E] = lo

        @pl.loop(0, CB + 2)
        def _(i):
            r0 = pl.multiple_of(i * BAND, BAND)
            y = dot(lmt[pl.ds(r0, BAND), :], cat_d[...])
            wext[pl.ds(r0, BAND), :] = weight * (y[:, :E] + y[:, E:])

        @pl.when(has_l)
        def _():
            wcopy_l(it).start()

        @pl.when(has_r)
        def _():
            wcopy_r(it).start()

    def reg_end(it):
        a[...] += wext[BAND:BAND + cols, :]

        @pl.when(has_l)
        def _():
            wcopy_r(it).wait_recv()

        @pl.when(has_r)
        def _():
            wcopy_l(it).wait_recv()

        a[0:BAND, :] += wr[it, 0]
        a[cols - BAND:cols, :] += wr[it, 1]

        @pl.when(has_l)
        def _():
            wcopy_l(it).wait_send()

        @pl.when(has_r)
        def _():
            wcopy_r(it).wait_send()

    def scopy(it, slot, q):
        return rcopy(scs.at[it], scr.at[it, slot], (sem_s.at[0, it, q], sem_s.at[1, it, slot]), at(obs, q))

    def sums_start(it):
        scr[it, pat] = scs[it]

        @pl.loop(1, n_patch)
        def _(i):
            scopy(it, pat, (pat + i) % n_patch).start()

    def sums_end(it):
        @pl.loop(1, n_patch)
        def _(i):
            q = (pat + i) % n_patch
            scopy(it, q, q).wait_recv()

        @pl.loop(1, n_patch)
        def _(i):
            q = (pat + i) % n_patch
            scopy(it, pat, q).wait_send()

        return jnp.sum(scr[it], axis=0)

    def pcopy(slot, i):
        o, q = plane(i)
        return rcopy(pls, plr.at[slot], (sem_p.at[i], sem_n.at[slot]), (o, q))

    def rowsum(x):
        return jnp.sum(x, axis=0, keepdims=True)

    norms = []

    def dots(it):
        gv, dv, av = g[...], d[...], a[...]
        scs[it, 0:1, :] = rowsum(gv * gv)
        scs[it, 1:2, :] = rowsum(dv * av)
        scs[it, 2:3, :] = rowsum(gv * av)
        scs[it, 3:4, :] = rowsum(av * av)
        sums_start(it)

    def first():
        halo_wait(0)
        hg[...] = hal[0]
        hd[...] = hal[0]

    def advance(it):
        tot = sums_end(it - 1)
        if it == 1:
            norms.append(tot[0:1])
        norm = norms[-1]
        step = norm / tot[1:2]
        after = norm - 2.0 * step * tot[2:3] + step * step * tot[3:4]
        ratio = after / norm
        norms.append(after)
        halo_wait(it)
        if it == 1:
            slip[...] = step * d[...]
        else:
            slip[...] += step * d[...]
        g[...] = g[...] - step * a[...]
        d[...] = g[...] + ratio * d[...]
        hg[...] = hg[...] - step * hal[it]
        hd[...] = hg[...] + ratio * hd[...]
        if it == ITERS - 1:
            laplace()

            @pl.loop(0, CB)
            def _(i):
                _, u = lap_rows(i)
                scs[it] += jnp.sum((u * u).reshape(BAND // 8, 8, E), axis=0)

            sums_start(it)
        return step, ratio

    backward(0, build_laplace, g)
    d[...] = g[...]
    forward(0, lambda: None, first)
    for it in range(1, ITERS):
        backward(it, functools.partial(reg_start, it - 1), a)
        reg_end(it - 1)
        forward(it, functools.partial(dots, it - 1), functools.partial(advance, it))
    last = ITERS - 1
    norm = norms[-1]
    me = obs * 2 + c
    pls[...] = sq[...]
    plr[me] = sq[...]

    @pl.loop(1, n_plane)
    def _(i):
        pcopy(me, i).start()

    reg = rowsum(sums_end(last))

    @pl.loop(1, n_plane)
    def _(i):
        pcopy((me + i) % n_plane, i).wait_recv()

    curvature = rowsum(jnp.sum(plr[...], axis=0)) + reg
    out[...] = slip[...] + (norm / curvature) * d[...]

    @pl.loop(1, n_plane)
    def _(i):
        pcopy(me, i).wait_send()


def shards(green, data, neighbours, reg_weight):
    rows, cols = green.shape
    E = data.shape[1]
    n_obs, n_patch = lax.axis_size("obs"), lax.axis_size("patch")
    nbit = n_obs.bit_length() - 1
    nc = rows // 2 // 64
    bc = 8
    R, BR, ext = rows // 2 // nc, cols // bc, cols + 2 * BAND
    V = pltpu.VMEM
    D = pltpu.SemaphoreType.DMA
    scratch = [
        V((rows, cols), BF16), V((rows, cols), BF16),
        V((cols, rows), BF16), V((cols, rows), BF16),
        V((cols, ext), BF16), V((ext, cols), BF16),
        V((cols, 2 * E), BF16), V((rows, 2 * E), BF16), V((ext, 2 * E), BF16),
        V((cols, E), F32), V((cols, E), F32), V((cols, E), F32), V((ext, E), F32), V((cols, E), F32),
        V((8, E), F32),
        V((2, BAND, E), F32), V((2, BAND, E), F32), V((nc, R, E), F32), V((nc, R, E), F32),
        V((nc, R, E), F32), V((nc, R, E), F32), V((ITERS, nc, R, E), F32),
        V((nc, R, E), F32), V((nc, R, E), F32),
        V((ITERS, nc, R, E), F32), V((ITERS, nc, R, E), F32),
        V((ITERS - 1, 2, nc, R, E), F32),
        V((ITERS, nbit, bc, BR, E), F32), V((ITERS, nbit, bc, BR, E), F32),
        V((ITERS, 2, BAND, E), F32), V((ITERS - 1, 2, BAND, E), F32),
        V((ITERS, 8, E), F32), V((ITERS, n_patch, 8, E), F32),
        V((8, E), F32), V((2 * n_obs, 8, E), F32),
        D((2, ITERS, nc)), D((2, ITERS, nc)), D((2, ITERS, nc)), D((2, ITERS - 1, nc)),
        D((2, ITERS, nbit, bc)), D((2, ITERS, 2)), D((2, ITERS - 1, 2)),
        D((2, ITERS, n_patch)), D((2 * n_obs,)), D((2 * n_obs,)),
    ]
    return pl.pallas_call(
        functools.partial(kernel, n_obs, n_patch, nc, bc),
        out_shape=jax.ShapeDtypeStruct((cols, E), F32),
        in_specs=[pl.BlockSpec(memory_space=pltpu.VMEM)] * 4,
        out_specs=pl.BlockSpec(memory_space=pltpu.VMEM),
        scratch_shapes=scratch,
        compiler_params=pltpu.CompilerParams(
            collective_id=0, has_side_effects=True, vmem_limit_bytes=56 * 1024 * 1024),
    )(green, data, neighbours, reg_weight.reshape(1, E))


def solution(mesh):
    in_specs = (P("obs", "patch"), P("obs", None), P(None, "patch"), P())
    return jax.shard_map(shards, mesh=mesh, in_specs=in_specs, out_specs=P("patch", None), check_vma=False)
```

profile of v0, /device:TPU:1, one launch (start us, length us, event | category | flops | bytes accessed | tf_op | source)
XLA Modules:
  0.0 268.5 jit_solution(14717130325694933102)
XLA Ops:
  0.0 266.8 %shard_map.46 = f32[640,128]{1,0:T(8,128)} custom-call(f32[1280,640]{1,0:T(8,128)} %green.1, f32[1280,128]{1,0:T(8,128)} %data.1, s32[3,640]{1,0:T(4,128)} %nb.1, f32[1,128]{1,0:T(1,128)} %bitcast.1), custom_call_target="tpu_custom_call" | custom-call | tf_op jit(solution)/shard_map/pallas_call | solution.py:523
  266.8 1.7 copy.6
where the time goes:
time: 269 us
  Pallas kernels  267 us (99%)
    pallas_call x1, Pallas kernels, shards(): pl.pallas_call(functools.partial(kernel, n_obs, n_patch, nc, bc), out_sha...  267 us

commit v1 on v0

v1 whole, which is shorter than its diff:
```python
import functools
import math

import jax
import jax.numpy as jnp
from jax import lax
from jax.experimental import pallas as pl
from jax.experimental.pallas import tpu as pltpu
from jax.sharding import PartitionSpec as P

BAND = 128
ITERS = 3
MESH = pl.DeviceIdType.MESH
F32 = jnp.float32
BF16 = jnp.bfloat16


def dot(a, b):
    return lax.dot_general(a, b, (((1,), (0,)), ((), ())), preferred_element_type=F32)


def split(x):
    hi = x.astype(BF16)
    return hi, (x - hi.astype(F32)).astype(BF16)


def kernel(n_obs, n_patch, green, data, nb, rw, out,
           ghi, glo, gthi, gtlo, lm, lmt, cat_d, cat_r, cat_e,
           d, g, a, wext, slip, hd, hg, qd, qg,
           pf, s, rd, zr, zrel, zfin, img, bs, br, ag, hal, wr, scs, scr, pls, plr, qls, qlr,
           sem_d, sem_z, sem_f, sem_g, sem_i, sem_b, sem_a, sem_h, sem_w, sem_s, sem_p, sem_q):
    rows, cols = green.shape
    E = data.shape[1]
    nz = n_patch // 2
    R = rows // 2 // nz
    BR = cols // n_obs
    half = rows // 2
    per = 4
    nch = n_obs // per
    nd = rd.shape[1]
    PD = nz // nd
    CB = cols // BAND
    Q = nz // 4
    plus = list(range(1, Q + 1))
    minus = list(range(1, Q))
    obs = lax.axis_index("obs")
    pat = lax.axis_index("patch")
    z = pat // 2
    c = pat % 2
    other = 1 - c
    partner = z * 2 + other
    has_l, has_r = pat > 0, pat < n_patch - 1
    weight = rw[...]

    def at(o, q):
        return (o, q)

    def rcopy(src, dst, sems, dev):
        return pltpu.make_async_remote_copy(
            src_ref=src, dst_ref=dst, send_sem=sems[0], recv_sem=sems[1],
            device_id=dev, device_id_type=MESH)

    def pair(sem, *idx):
        return sem.at[(0,) + idx], sem.at[(1,) + idx]

    barrier = pltpu.get_barrier_semaphore()

    @pl.loop(1, n_patch)
    def _(i):
        pl.semaphore_signal(barrier, inc=1, device_id=at(obs, (pat + i) % n_patch), device_id_type=MESH)

    @pl.loop(1, n_obs)
    def _(i):
        pl.semaphore_signal(barrier, inc=1, device_id=at((obs + i) % n_obs, pat), device_id_type=MESH)

    nblk = rows // BAND

    @pl.loop(0, nblk)
    def _(i):
        r0 = pl.multiple_of(i * BAND, BAND)
        block = green[pl.ds(r0, BAND), :]
        hi, lo = split(block)
        ghi[pl.ds(r0, BAND), :] = hi
        glo[pl.ds(r0, BAND), :] = lo
        hi, lo = split(block.T)
        gthi[:, pl.ds(r0, BAND)] = hi
        gtlo[:, pl.ds(r0, BAND)] = lo
        hi, lo = split(data[pl.ds(r0, BAND), :])
        cat_r[pl.ds(r0, BAND), 0:E] = hi
        cat_r[pl.ds(r0, BAND), E:2 * E] = lo

    scs[...] = jnp.zeros((ITERS, 8, E), F32)
    zero_h = jnp.zeros((BAND, E), F32)

    @pl.when(pat == 0)
    def _():
        for it in range(ITERS):
            hal[it, 0] = zero_h
        for it in range(ITERS - 1):
            wr[it, 0] = zero_h

    @pl.when(pat == n_patch - 1)
    def _():
        for it in range(ITERS):
            hal[it, 1] = zero_h
        for it in range(ITERS - 1):
            wr[it, 1] = zero_h

    def build_laplace():
        @pl.loop(0, CB + 2)
        def _(j):
            r0 = pl.multiple_of(j * BAND, BAND)
            col = lax.broadcasted_iota(jnp.int32, (BAND, cols), 0) + j * BAND
            own = lax.broadcasted_iota(jnp.int32, (BAND, cols), 1) + BAND
            m = jnp.where(col == own, 4.0, 0.0)
            col = col + (pat * cols - BAND)
            for k in range(3):
                m = m - jnp.where(col == nb[k:k + 1, :], 1.0, 0.0)
            lmt[pl.ds(r0, BAND), :] = m.astype(BF16)
            lm[:, pl.ds(r0, BAND)] = m.T.astype(BF16)

    pl.semaphore_wait(barrier, n_patch - 1 + n_obs - 1)

    def bcopy(b, o, slot):
        return rcopy(bs.at[b, o], br.at[b, slot], (sem_b.at[0, b, o], sem_b.at[1, b, slot]), at(o, pat))

    def acopy(b, o, slot):
        r0 = pl.multiple_of(slot * BR, BR)
        return rcopy(ag.at[b, pl.ds(r0, BR)], ag.at[b, pl.ds(r0, BR)],
                     (sem_a.at[0, b, o], sem_a.at[1, b, slot]), at(o, pat))

    def backward(b, hook):
        @pl.loop(1, nch + 1)
        def _(j):
            ch = (obs // per + j) % nch
            r0 = pl.multiple_of(ch * (per * BR), per * BR)
            y = dot(gthi[pl.ds(r0, per * BR), :], cat_r[...])
            y = y[:, :E] + y[:, E:] + dot(gtlo[pl.ds(r0, per * BR), :], cat_r[:, 0:E])
            bs[b, pl.ds(ch * per, per)] = y.reshape(per, BR, E)
            for i in range(per):
                o = ch * per + i

                @pl.when(o != obs)
                def _():
                    bcopy(b, o, obs).start()

        hook()

        def add(i, acc):
            o = (obs + i) % n_obs
            bcopy(b, o, o).wait_recv()
            return acc + br[b, o]

        total = lax.fori_loop(1, n_obs, add, bs[b, obs])
        ag[b, pl.ds(pl.multiple_of(obs * BR, BR), BR), :] = total

        @pl.loop(1, n_obs)
        def _(i):
            acopy(b, (obs + i) % n_obs, obs).start()

        @pl.loop(1, n_obs)
        def _(i):
            o = (obs + i) % n_obs
            acopy(b, o, o).wait_recv()

    def backward_end(b):
        @pl.loop(1, n_obs)
        def _(i):
            o = (obs + i) % n_obs
            bcopy(b, o, obs).wait_send()
            acopy(b, o, obs).wait_send()

    def dcopy(it, k):
        return rcopy(pf.at[pl.ds(k * PD, PD)], rd.at[it, k], pair(sem_d, it, k), at(obs, partner))

    def zat(k):
        return at(obs, ((z + k + nz) % nz) * 2 + c)

    def owner(k):
        return (z + k + 2 * nz) % nz

    first_step = ([(-k, -k - Q) for k in reversed(plus)] + [(k, k + Q) for k in reversed(minus)]
                  + [(-k, -k) for k in reversed(minus)] + [(k, k) for k in reversed(minus)])
    n_plus, n_minus = len(plus), len(minus)

    def zcopy(it, slot):
        k, o = first_step[slot]
        return rcopy(s.at[owner(o)], zr.at[it, slot], pair(sem_z, it, slot), zat(k))

    def fcopy(it, slot):
        return rcopy(zrel.at[slot], zfin.at[it, slot], pair(sem_f, it, slot), zat(-Q if slot == 0 else Q))

    near = [(k, 0) for k in (-Q, Q) ] + [(sgn * k, 0) for k in reversed(minus) for sgn in (1, -1)]
    relay_p = [(k, -Q) for k in reversed(plus)]
    relay_m = [(-k, Q) for k in reversed(minus)]
    gather = near + relay_p + relay_m

    def gcopy(it, m):
        k, o = gather[m]
        p = owner(o)
        return rcopy(img.at[it, c, p], img.at[it, c, p], (sem_g.at[0, it, m], sem_g.at[1, it, p]), zat(k))

    def gwait(it, p):
        rcopy(img.at[it, c, p], img.at[it, c, p], (sem_g.at[0, it, 0], sem_g.at[1, it, p]), zat(1)).wait_recv()

    def icopy(it, k):
        return rcopy(img.at[it, c, k], img.at[it, c, k], pair(sem_i, it, k), at(obs, partner))

    def fold(acc, it, slots):
        for slot in slots:
            zcopy(it, slot).wait_recv()
            acc = acc + zr[it, slot]
        return acc

    def hsrc(it):
        return a if it else ag.at[0]

    def hcopy_r(it):
        return rcopy(hsrc(it).at[pl.ds(cols - BAND, BAND)], hal.at[it, 0], pair(sem_h, it, 0), at(obs, pat + 1))

    def hcopy_l(it):
        return rcopy(hsrc(it).at[pl.ds(0, BAND)], hal.at[it, 1], pair(sem_h, it, 1), at(obs, pat - 1))

    def forward(it, sums, hook):
        last = it == ITERS - 1

        hi, lo = split(hsrc(it)[...])
        cat_d[:, 0:E] = hi
        cat_d[:, E:2 * E] = lo

        def part(h):
            r0 = pl.multiple_of(h * half, half)
            y = dot(ghi[pl.ds(r0, half), :], cat_d[...])
            y = y[:, :E] + y[:, E:] + dot(glo[pl.ds(r0, half), :], cat_d[:, 0:E])
            return y.reshape(nz, R, E)

        pf[...] = part(other)

        for k in range(nd):
            dcopy(it, k).start()

        @pl.when(has_r)
        def _():
            hcopy_r(it).start()

        @pl.when(has_l)
        def _():
            hcopy_l(it).start()

        s[...] = part(c)
        sums()

        for k in range(nd):
            dcopy(it, k).wait_recv()
            s[k * PD:(k + 1) * PD] += rd[it, k]

        for slot in range(len(first_step)):
            zcopy(it, slot).start()

        zrel[0] = fold(s[owner(-Q)], it, range(n_plus))
        fcopy(it, 0).start()
        zrel[1] = fold(s[owner(Q)], it, range(n_plus, n_plus + n_minus))
        fcopy(it, 1).start()

        scalars = hook()

        total = fold(s[z], it, range(n_plus + n_minus, len(first_step)))
        for slot in range(2):
            fcopy(it, slot).wait_recv()
            total = total + zfin[it, slot]

        if it:
            step, ratio = scalars
            rest = qg[...] - step * total
            total = rest + ratio * qd[...]
        else:
            rest = total
        if last:
            sq = jnp.sum((total * total).reshape(R // 8, 8, E), axis=0)
        else:
            sq = None
            qg[...] = rest
            qd[...] = total
            img[it, c, z] = total
            for m in range(len(near)):
                gcopy(it, m).start()
            icopy(it, z).start()
            gwait(it, owner(-Q))
            for m in range(len(near), len(near) + len(relay_p)):
                gcopy(it, m).start()
            gwait(it, owner(Q))
            for m in range(len(near) + len(relay_p), len(gather)):
                gcopy(it, m).start()
            icopy(it, owner(-Q)).start()
            icopy(it, owner(Q)).start()
            seen = {0, nz - Q, Q}
            for k in minus:
                for o in (-k, k):
                    gwait(it, owner(o))
                    icopy(it, owner(o)).start()
                    seen.add(o % nz)
            for o in range(nz):
                if o not in seen:
                    gwait(it, owner(o))
                    icopy(it, owner(o)).start()
            for o in range(nz):
                icopy(it, owner(o)).wait_recv()
            hi, lo = split(img[it].reshape(rows, E))
            cat_r[:, 0:E] = hi
            cat_r[:, E:2 * E] = lo

        return sq

    def forward_end(it):
        for k in range(nd):
            dcopy(it, k).wait_send()
        for slot in range(len(first_step)):
            zcopy(it, slot).wait_send()
        for slot in range(2):
            fcopy(it, slot).wait_send()
        if it < ITERS - 1:
            for m in range(len(gather)):
                gcopy(it, m).wait_send()

            @pl.loop(0, nz)
            def _(k):
                icopy(it, k).wait_send()

    def halo_wait(it):
        @pl.when(has_l)
        def _():
            hcopy_r(it).wait_recv()

        @pl.when(has_r)
        def _():
            hcopy_l(it).wait_recv()

        @pl.when(has_r)
        def _():
            hcopy_r(it).wait_send()

        @pl.when(has_l)
        def _():
            hcopy_l(it).wait_send()

    def laplace():
        for r0, n, v in ((0, BAND, hd[0]), (BAND, cols, d[...]), (BAND + cols, BAND, hd[1])):
            hi, lo = split(v)
            cat_e[r0:r0 + n, 0:E] = hi
            cat_e[r0:r0 + n, E:2 * E] = lo

    def lap_rows(i):
        r0 = pl.multiple_of(i * BAND, BAND)
        y = dot(lm[pl.ds(r0, BAND), :], cat_e[...])
        return r0, weight * (y[:, :E] + y[:, E:])

    def wcopy_l(it):
        return rcopy(wext.at[pl.ds(0, BAND)], wr.at[it, 1], pair(sem_w, it, 1), at(obs, pat - 1))

    def wcopy_r(it):
        return rcopy(wext.at[pl.ds(BAND + cols, BAND)], wr.at[it, 0], pair(sem_w, it, 0), at(obs, pat + 1))

    def reg_start(it):
        laplace()

        @pl.loop(0, CB)
        def _(i):
            r0, u = lap_rows(i)
            hi, lo = split(u)
            cat_d[pl.ds(r0, BAND), 0:E] = hi
            cat_d[pl.ds(r0, BAND), E:2 * E] = lo

        @pl.loop(0, CB + 2)
        def _(i):
            r0 = pl.multiple_of(i * BAND, BAND)
            y = dot(lmt[pl.ds(r0, BAND), :], cat_d[...])
            wext[pl.ds(r0, BAND), :] = weight * (y[:, :E] + y[:, E:])

        @pl.when(has_l)
        def _():
            wcopy_l(it).start()

        @pl.when(has_r)
        def _():
            wcopy_r(it).start()

    def reg_end(it):
        a[...] = ag[it + 1] + wext[BAND:BAND + cols, :]

        @pl.when(has_l)
        def _():
            wcopy_r(it).wait_recv()

        @pl.when(has_r)
        def _():
            wcopy_l(it).wait_recv()

        a[0:BAND, :] += wr[it, 0]
        a[cols - BAND:cols, :] += wr[it, 1]

    def reg_done(it):
        @pl.when(has_l)
        def _():
            wcopy_l(it).wait_send()

        @pl.when(has_r)
        def _():
            wcopy_r(it).wait_send()

    def scopy(it, slot, q):
        return rcopy(scs.at[it], scr.at[it, slot], (sem_s.at[0, it, q], sem_s.at[1, it, slot]), at(obs, q))

    def sums_start(it):
        scr[it, pat] = scs[it]

        @pl.loop(1, n_patch)
        def _(i):
            scopy(it, pat, (pat + i) % n_patch).start()

    def sums_end(it):
        @pl.loop(1, n_patch)
        def _(i):
            q = (pat + i) % n_patch
            scopy(it, q, q).wait_recv()

        @pl.loop(1, n_patch)
        def _(i):
            q = (pat + i) % n_patch
            scopy(it, pat, q).wait_send()

        return jnp.sum(scr[it], axis=0)

    def pcopy(q, slot):
        return rcopy(pls, plr.at[slot], (sem_p.at[0, q], sem_p.at[1, slot]), at(obs, q))

    def qcopy(o, slot):
        return rcopy(qls, qlr.at[slot], (sem_q.at[0, o], sem_q.at[1, slot]), at(o, pat))

    def rowsum(x):
        return jnp.sum(x, axis=0, keepdims=True)

    norms = []

    def dots(it):
        gv, dv, av = g[...], d[...], a[...]
        scs[it, 0:1, :] = rowsum(gv * gv)
        scs[it, 1:2, :] = rowsum(dv * av)
        scs[it, 2:3, :] = rowsum(gv * av)
        scs[it, 3:4, :] = rowsum(av * av)
        sums_start(it)

    def first():
        halo_wait(0)
        hg[...] = hal[0]
        hd[...] = hal[0]

    def advance(it):
        tot = sums_end(it - 1)
        if it == 1:
            norms.append(tot[0:1])
        norm = norms[-1]
        step = norm / tot[1:2]
        after = norm - 2.0 * step * tot[2:3] + step * step * tot[3:4]
        ratio = after / norm
        norms.append(after)
        halo_wait(it)
        if it == 1:
            slip[...] = step * d[...]
        else:
            slip[...] += step * d[...]
        g[...] = g[...] - step * a[...]
        d[...] = g[...] + ratio * d[...]
        hg[...] = hg[...] - step * hal[it]
        hd[...] = hg[...] + ratio * hd[...]
        if it == ITERS - 1:
            laplace()

            @pl.loop(0, CB)
            def _(i):
                _, u = lap_rows(i)
                scs[it] += jnp.sum((u * u).reshape(BAND // 8, 8, E), axis=0)

            sums_start(it)
        return step, ratio

    backward(0, build_laplace)
    g[...] = ag[0]
    d[...] = ag[0]
    forward(0, lambda: None, first)
    for it in range(1, ITERS):
        backward(it, functools.partial(reg_start, it - 1))
        forward_end(it - 1)
        reg_end(it - 1)
        sq = forward(it, functools.partial(dots, it - 1), functools.partial(advance, it))
        reg_done(it - 1)
    last = ITERS - 1
    norm = norms[-1]
    pls[...] = sq
    plr[pat] = sq

    @pl.loop(1, n_patch)
    def _(i):
        pcopy((pat + i) % n_patch, pat).start()

    reg = rowsum(sums_end(last))
    forward_end(last)
    for it in range(ITERS):
        backward_end(it)

    @pl.loop(1, n_patch)
    def _(i):
        q = (pat + i) % n_patch
        pcopy(q, q).wait_recv()

    part = jnp.sum(plr[...], axis=0)
    qls[...] = part
    qlr[obs] = part

    @pl.loop(1, n_obs)
    def _(i):
        qcopy((obs + i) % n_obs, obs).start()

    @pl.loop(1, n_patch)
    def _(i):
        pcopy((pat + i) % n_patch, pat).wait_send()

    @pl.loop(1, n_obs)
    def _(i):
        o = (obs + i) % n_obs
        qcopy(o, o).wait_recv()

    curvature = rowsum(jnp.sum(qlr[...], axis=0)) + reg
    out[...] = slip[...] + (norm / curvature) * d[...]

    @pl.loop(1, n_obs)
    def _(i):
        qcopy((obs + i) % n_obs, obs).wait_send()


def shards(green, data, neighbours, reg_weight):
    rows, cols = green.shape
    E = data.shape[1]
    n_obs, n_patch = lax.axis_size("obs"), lax.axis_size("patch")
    nz = n_patch // 2
    nd = 4
    R, BR, ext = rows // 2 // nz, cols // n_obs, cols + 2 * BAND
    first, messages = 4 * (nz // 4) - 3, nz - 1
    V = pltpu.VMEM
    D = pltpu.SemaphoreType.DMA
    scratch = [
        V((rows, cols), BF16), V((rows, cols), BF16),
        V((cols, rows), BF16), V((cols, rows), BF16),
        V((cols, ext), BF16), V((ext, cols), BF16),
        V((cols, 2 * E), BF16), V((rows, 2 * E), BF16), V((ext, 2 * E), BF16),
        V((cols, E), F32), V((cols, E), F32), V((cols, E), F32), V((ext, E), F32), V((cols, E), F32),
        V((2, BAND, E), F32), V((2, BAND, E), F32), V((R, E), F32), V((R, E), F32),
        V((nz, R, E), F32), V((nz, R, E), F32), V((ITERS, nd, nz // nd, R, E), F32),
        V((ITERS, first, R, E), F32), V((2, R, E), F32), V((ITERS, 2, R, E), F32),
        V((ITERS - 1, 2, nz, R, E), F32),
        V((ITERS, n_obs, BR, E), F32), V((ITERS, n_obs, BR, E), F32), V((ITERS, cols, E), F32),
        V((ITERS, 2, BAND, E), F32), V((ITERS - 1, 2, BAND, E), F32),
        V((ITERS, 8, E), F32), V((ITERS, n_patch, 8, E), F32),
        V((8, E), F32), V((n_patch, 8, E), F32), V((8, E), F32), V((n_obs, 8, E), F32),
        D((2, ITERS, nd)), D((2, ITERS, first)), D((2, ITERS, 2)), D((2, ITERS - 1, nz)), D((2, ITERS - 1, nz)),
        D((2, ITERS, n_obs)), D((2, ITERS, n_obs)), D((2, ITERS, 2)), D((2, ITERS - 1, 2)),
        D((2, ITERS, n_patch)), D((2, n_patch)), D((2, n_obs)),
    ]
    return pl.pallas_call(
        functools.partial(kernel, n_obs, n_patch),
        out_shape=jax.ShapeDtypeStruct((cols, E), F32),
        in_specs=[pl.BlockSpec(memory_space=pltpu.VMEM)] * 4,
        out_specs=pl.BlockSpec(memory_space=pltpu.VMEM),
        scratch_shapes=scratch,
        compiler_params=pltpu.CompilerParams(
            collective_id=0, has_side_effects=True, vmem_limit_bytes=56 * 1024 * 1024),
    )(green, data, neighbours, reg_weight.reshape(1, E))


def solution(mesh):
    in_specs = (P("obs", "patch"), P("obs", None), P(None, "patch"), P())
    return jax.shard_map(shards, mesh=mesh, in_specs=in_specs, out_specs=P("patch", None), check_vma=False)
```

time: 269 us -> 171 us (0.64)
  Pallas kernels: 267 us -> 169 us
    pallas_call x1, Pallas kernels: 267 us -> 169 us  [shards(): pl.pallas_call(functools.partial(kernel, n_obs, n_patch), out_shape=jax.S...]
where the time goes in v1:
time: 171 us; the launch traced here: 170 us
  Pallas kernels  169 us (99%)
  local copies, waits for them, and re-layouts  1.72 us (1%)
    pallas_call x1, Pallas kernels, shards(): pl.pallas_call(functools.partial(kernel, n_obs, n_patch), out_shape=jax.S...  169 us

profile of v1, /device:TPU:1, one launch (start us, length us, event | category | flops | bytes accessed | tf_op | source)
XLA Modules:
  0.0 170.4 jit_solution(15438277010196042925)
XLA Ops:
  0.0 168.7 %shard_map.46 = f32[640,128]{1,0:T(8,128)} custom-call(f32[1280,640]{1,0:T(8,128)} %green.1, f32[1280,128]{1,0:T(8,128)} %data.1, s32[3,640]{1,0:T(4,128)} %nb.1, f32[1,128]{1,0:T(1,128)} %bitcast.1), custom_call_target="tpu_custom_call" | custom-call | tf_op jit(solution)/shard_map/pallas_call | solution.py:568
  168.7 1.7 %copy.6 = f32[640,128]{1,0:T(8,128)} copy(f32[640,128]{1,0:T(8,128)} %shard_map.46) | data formatting | bytes 655360

commit v2 on v1

--- a/solution.py
+++ b/solution.py
@@ -24,11 +24,12 @@
     return hi, (x - hi.astype(F32)).astype(BF16)
 
 
-def kernel(n_obs, n_patch, green, data, nb, rw, out,
+def kernel(n_obs, n_patch, green_h, data_h, nb_h, rw_h, slip_h, d_h, scale,
+           green, data, nb, rw,
            ghi, glo, gthi, gtlo, lm, lmt, cat_d, cat_r, cat_e,
            d, g, a, wext, slip, hd, hg, qd, qg,
-           pf, s, rd, zr, zrel, zfin, img, bs, br, ag, hal, wr, scs, scr, pls, plr, qls, qlr,
-           sem_d, sem_z, sem_f, sem_g, sem_i, sem_b, sem_a, sem_h, sem_w, sem_s, sem_p, sem_q):
+           pf, s, rd, zr, zrel, zfin, img, bs, br, ag, hal, wr, scs, scp, scz, scr, pls, plr, qls, qlr,
+           sem_l, sem_o, sem_d, sem_z, sem_f, sem_g, sem_i, sem_b, sem_a, sem_h, sem_w, sem_c, sem_s, sem_p, sem_q):
     rows, cols = green.shape
     E = data.shape[1]
     nz = n_patch // 2
@@ -50,7 +51,6 @@
     other = 1 - c
     partner = z * 2 + other
     has_l, has_r = pat > 0, pat < n_patch - 1
-    weight = rw[...]
 
     def at(o, q):
         return (o, q)
@@ -63,6 +63,23 @@
     def pair(sem, *idx):
         return sem.at[(0,) + idx], sem.at[(1,) + idx]
 
+    nblk = rows // BAND
+
+    def load(i):
+        r0 = pl.multiple_of(i * BAND, BAND)
+        return pltpu.make_async_copy(green_h.at[pl.ds(r0, BAND)], green.at[pl.ds(r0, BAND)], sem_l.at[i])
+
+    small = [pltpu.make_async_copy(src, dst, sem_l.at[nblk + i])
+             for i, (src, dst) in enumerate(((data_h, data), (nb_h, nb), (rw_h, rw)))]
+    small[0].start()
+
+    @pl.loop(0, nblk)
+    def _(i):
+        load(i).start()
+
+    for copy in small[1:]:
+        copy.start()
+
     barrier = pltpu.get_barrier_semaphore()
 
     @pl.loop(1, n_patch)
@@ -73,11 +90,12 @@
     def _(i):
         pl.semaphore_signal(barrier, inc=1, device_id=at((obs + i) % n_obs, pat), device_id_type=MESH)
 
-    nblk = rows // BAND
+    small[0].wait()
 
     @pl.loop(0, nblk)
     def _(i):
         r0 = pl.multiple_of(i * BAND, BAND)
+        load(i).wait()
         block = green[pl.ds(r0, BAND), :]
         hi, lo = split(block)
         ghi[pl.ds(r0, BAND), :] = hi
@@ -89,7 +107,10 @@
         cat_r[pl.ds(r0, BAND), 0:E] = hi
         cat_r[pl.ds(r0, BAND), E:2 * E] = lo
 
-    scs[...] = jnp.zeros((ITERS, 8, E), F32)
+    for copy in small[1:]:
+        copy.wait()
+    weight = rw[...]
+
     zero_h = jnp.zeros((BAND, E), F32)
 
     @pl.when(pat == 0)
@@ -119,8 +140,6 @@
             lmt[pl.ds(r0, BAND), :] = m.astype(BF16)
             lm[:, pl.ds(r0, BAND)] = m.T.astype(BF16)
 
-    pl.semaphore_wait(barrier, n_patch - 1 + n_obs - 1)
-
     def bcopy(b, o, slot):
         return rcopy(bs.at[b, o], br.at[b, slot], (sem_b.at[0, b, o], sem_b.at[1, b, slot]), at(o, pat))
 
@@ -137,6 +156,8 @@
             y = dot(gthi[pl.ds(r0, per * BR), :], cat_r[...])
             y = y[:, :E] + y[:, E:] + dot(gtlo[pl.ds(r0, per * BR), :], cat_r[:, 0:E])
             bs[b, pl.ds(ch * per, per)] = y.reshape(per, BR, E)
+            if b == 0:
+                return
             for i in range(per):
                 o = ch * per + i
 
@@ -145,6 +166,13 @@
                     bcopy(b, o, obs).start()
 
         hook()
+
+        if b == 0:
+            pl.semaphore_wait(barrier, n_patch - 1 + n_obs - 1)
+
+            @pl.loop(1, n_obs)
+            def _(i):
+                bcopy(b, (obs + i) % n_obs, obs).start()
 
         def add(i, acc):
             o = (obs + i) % n_obs
@@ -221,7 +249,7 @@
     def hcopy_l(it):
         return rcopy(hsrc(it).at[pl.ds(0, BAND)], hal.at[it, 1], pair(sem_h, it, 1), at(obs, pat - 1))
 
-    def forward(it, sums, hook):
+    def forward(it, hook):
         last = it == ITERS - 1
 
         hi, lo = split(hsrc(it)[...])
@@ -239,22 +267,30 @@
         for k in range(nd):
             dcopy(it, k).start()
 
-        @pl.when(has_r)
-        def _():
-            hcopy_r(it).start()
-
-        @pl.when(has_l)
-        def _():
-            hcopy_l(it).start()
+        if it:
+            dots(it - 1)
 
         s[...] = part(c)
-        sums()
 
         for k in range(nd):
             dcopy(it, k).wait_recv()
             s[k * PD:(k + 1) * PD] += rd[it, k]
 
-        for slot in range(len(first_step)):
+        for slot in range(n_plus + n_minus):
+            zcopy(it, slot).start()
+
+        if it:
+            sums_mid(it - 1)
+
+        @pl.when(has_r)
+        def _():
+            hcopy_r(it).start()
+
+        @pl.when(has_l)
+        def _():
+            hcopy_l(it).start()
+
+        for slot in range(n_plus + n_minus, len(first_step)):
             zcopy(it, slot).start()
 
         zrel[0] = fold(s[owner(-Q)], it, range(n_plus))
@@ -275,8 +311,9 @@
             total = rest + ratio * qd[...]
         else:
             rest = total
+
         if last:
-            sq = jnp.sum((total * total).reshape(R // 8, 8, E), axis=0)
+            sq = jnp.sum(total * total, axis=0, keepdims=True)
         else:
             sq = None
             qg[...] = rest
@@ -294,6 +331,7 @@
             icopy(it, owner(-Q)).start()
             icopy(it, owner(Q)).start()
             seen = {0, nz - Q, Q}
+
             for k in minus:
                 for o in (-k, k):
                     gwait(it, owner(o))
@@ -303,6 +341,7 @@
                 if o not in seen:
                     gwait(it, owner(o))
                     icopy(it, owner(o)).start()
+
             for o in range(nz):
                 icopy(it, owner(o)).wait_recv()
             hi, lo = split(img[it].reshape(rows, E))
@@ -407,28 +446,34 @@
         def _():
             wcopy_r(it).wait_send()
 
-    def scopy(it, slot, q):
-        return rcopy(scs.at[it], scr.at[it, slot], (sem_s.at[0, it, q], sem_s.at[1, it, slot]), at(obs, q))
-
-    def sums_start(it):
-        scr[it, pat] = scs[it]
-
-        @pl.loop(1, n_patch)
-        def _(i):
-            scopy(it, pat, (pat + i) % n_patch).start()
+    def ccopy(it):
+        return rcopy(scs.at[it], scp.at[it], pair(sem_c, it), at(obs, partner))
+
+    def scopy(it, k, slot):
+        return rcopy(scz.at[it], scr.at[it, slot], (sem_s.at[0, it, k], sem_s.at[1, it, slot]), zat(k))
+
+    def sums_mid(it):
+        ccopy(it).wait_recv()
+        scz[it] = scs[it] + scp[it]
+        scr[it, z] = scs[it] + scp[it]
+
+        @pl.loop(1, nz)
+        def _(k):
+            scopy(it, k, z).start()
 
     def sums_end(it):
-        @pl.loop(1, n_patch)
-        def _(i):
-            q = (pat + i) % n_patch
-            scopy(it, q, q).wait_recv()
-
-        @pl.loop(1, n_patch)
-        def _(i):
-            q = (pat + i) % n_patch
-            scopy(it, pat, q).wait_send()
+        @pl.loop(1, nz)
+        def _(k):
+            scopy(it, k, owner(k)).wait_recv()
 
         return jnp.sum(scr[it], axis=0)
+
+    def sums_done(it):
+        ccopy(it).wait_send()
+
+        @pl.loop(1, nz)
+        def _(k):
+            scopy(it, k, z).wait_send()
 
     def pcopy(q, slot):
         return rcopy(pls, plr.at[slot], (sem_p.at[0, q], sem_p.at[1, slot]), at(obs, q))
@@ -439,7 +484,7 @@
     def rowsum(x):
         return jnp.sum(x, axis=0, keepdims=True)
 
-    norms = []
+    norms, regs = [], []
 
     def dots(it):
         gv, dv, av = g[...], d[...], a[...]
@@ -447,7 +492,7 @@
         scs[it, 1:2, :] = rowsum(dv * av)
         scs[it, 2:3, :] = rowsum(gv * av)
         scs[it, 3:4, :] = rowsum(av * av)
-        sums_start(it)
+        ccopy(it).start()
 
     def first():
         halo_wait(0)
@@ -475,26 +520,28 @@
         if it == ITERS - 1:
             laplace()
 
-            @pl.loop(0, CB)
-            def _(i):
+            def energy(i, acc):
                 _, u = lap_rows(i)
-                scs[it] += jnp.sum((u * u).reshape(BAND // 8, 8, E), axis=0)
-
-            sums_start(it)
+                return acc + jnp.sum((u * u).reshape(BAND // 8, 8, E), axis=0)
+
+            regs.append(rowsum(lax.fori_loop(0, CB, energy, jnp.zeros((8, E), F32))))
+            for k, (src, dst) in enumerate(((slip, slip_h), (d, d_h))):
+                pltpu.make_async_copy(src, dst, sem_o.at[k]).start()
         return step, ratio
 
     backward(0, build_laplace)
     g[...] = ag[0]
     d[...] = ag[0]
-    forward(0, lambda: None, first)
+    forward(0, first)
     for it in range(1, ITERS):
         backward(it, functools.partial(reg_start, it - 1))
         forward_end(it - 1)
         reg_end(it - 1)
-        sq = forward(it, functools.partial(dots, it - 1), functools.partial(advance, it))
+        sq = forward(it, functools.partial(advance, it))
         reg_done(it - 1)
     last = ITERS - 1
     norm = norms[-1]
+    sq = sq + jnp.where(obs == 0, regs[0], 0.0)
     pls[...] = sq
     plr[pat] = sq
 
@@ -502,19 +549,20 @@
     def _(i):
         pcopy((pat + i) % n_patch, pat).start()
 
-    reg = rowsum(sums_end(last))
     forward_end(last)
     for it in range(ITERS):
         backward_end(it)
+    for it in range(ITERS - 1):
+        sums_done(it)
 
     @pl.loop(1, n_patch)
     def _(i):
         q = (pat + i) % n_patch
         pcopy(q, q).wait_recv()
 
-    part = jnp.sum(plr[...], axis=0)
-    qls[...] = part
-    qlr[obs] = part
+    line = jnp.sum(plr[...], axis=0)
+    qls[...] = line
+    qlr[obs] = line
 
     @pl.loop(1, n_obs)
     def _(i):
@@ -523,14 +571,16 @@
     @pl.loop(1, n_patch)
     def _(i):
         pcopy((pat + i) % n_patch, pat).wait_send()
+
+    for k, (src, dst) in enumerate(((slip, slip_h), (d, d_h))):
+        pltpu.make_async_copy(src, dst, sem_o.at[k]).wait()
 
     @pl.loop(1, n_obs)
     def _(i):
         o = (obs + i) % n_obs
         qcopy(o, o).wait_recv()
 
-    curvature = rowsum(jnp.sum(qlr[...], axis=0)) + reg
-    out[...] = slip[...] + (norm / curvature) * d[...]
+    scale[...] = norm / jnp.sum(qlr[...], axis=0)
 
     @pl.loop(1, n_obs)
     def _(i):
@@ -548,6 +598,7 @@
     V = pltpu.VMEM
     D = pltpu.SemaphoreType.DMA
     scratch = [
+        V((rows, cols), F32), V((rows, E), F32), V(neighbours.shape, jnp.int32), V((1, E), F32),
         V((rows, cols), BF16), V((rows, cols), BF16),
         V((cols, rows), BF16), V((cols, rows), BF16),
         V((cols, ext), BF16), V((ext, cols), BF16),
@@ -559,21 +610,24 @@
         V((ITERS - 1, 2, nz, R, E), F32),
         V((ITERS, n_obs, BR, E), F32), V((ITERS, n_obs, BR, E), F32), V((ITERS, cols, E), F32),
         V((ITERS, 2, BAND, E), F32), V((ITERS - 1, 2, BAND, E), F32),
-        V((ITERS, 8, E), F32), V((ITERS, n_patch, 8, E), F32),
-        V((8, E), F32), V((n_patch, 8, E), F32), V((8, E), F32), V((n_obs, 8, E), F32),
+        V((ITERS - 1, 4, E), F32), V((ITERS - 1, 4, E), F32), V((ITERS - 1, 4, E), F32), V((ITERS - 1, nz, 4, E), F32),
+        V((1, E), F32), V((n_patch, 1, E), F32), V((1, E), F32), V((n_obs, 1, E), F32),
+        D((rows // BAND + 3,)), D((2,)),
         D((2, ITERS, nd)), D((2, ITERS, first)), D((2, ITERS, 2)), D((2, ITERS - 1, nz)), D((2, ITERS - 1, nz)),
         D((2, ITERS, n_obs)), D((2, ITERS, n_obs)), D((2, ITERS, 2)), D((2, ITERS - 1, 2)),
-        D((2, ITERS, n_patch)), D((2, n_patch)), D((2, n_obs)),
+        D((2, ITERS - 1)), D((2, ITERS - 1, nz)), D((2, n_patch)), D((2, n_obs)),
     ]
-    return pl.pallas_call(
+    anywhere = pl.BlockSpec(memory_space=pl.ANY)
+    slip, d, scale = pl.pallas_call(
         functools.partial(kernel, n_obs, n_patch),
-        out_shape=jax.ShapeDtypeStruct((cols, E), F32),
-        in_specs=[pl.BlockSpec(memory_space=pltpu.VMEM)] * 4,
-        out_specs=pl.BlockSpec(memory_space=pltpu.VMEM),
+        out_shape=[jax.ShapeDtypeStruct((cols, E), F32)] * 2 + [jax.ShapeDtypeStruct((1, E), F32)],
+        in_specs=[anywhere] * 4,
+        out_specs=[anywhere, anywhere, pl.BlockSpec(memory_space=pltpu.VMEM)],
         scratch_shapes=scratch,
         compiler_params=pltpu.CompilerParams(
             collective_id=0, has_side_effects=True, vmem_limit_bytes=56 * 1024 * 1024),
     )(green, data, neighbours, reg_weight.reshape(1, E))
+    return slip + scale * d
 
 
 def solution(mesh):

time: 171 us -> 152 us (0.89)
  Pallas kernels: 169 us -> 150 us
  other arithmetic: 0 us -> 1.83 us
  local copies, waits for them, and re-layouts: 1.72 us -> 0 us
    pallas_call x1, Pallas kernels: 169 us -> 150 us  [shards(): pl.pallas_call(functools.partial(kernel, n_obs, n_patch), out_shape=[jax....]
    add x0 -> x1, other arithmetic: none -> 1.83 us  [shards(): return slip + scale * d]
    unnamed x1 -> x0, local copies, waits for them, and re-layouts: 1.72 us -> none
where the time goes in v2:
time: 152 us
  Pallas kernels  150 us (99%)
  other arithmetic  1.83 us (1%)
    pallas_call x1, Pallas kernels, shards(): pl.pallas_call(functools.partial(kernel, n_obs, n_patch), out_shape=[jax....  150 us

profile of v2, /device:TPU:1, one launch (start us, length us, event | category | flops | bytes accessed | tf_op | source)
XLA Modules:
  0.0 152.0 jit_solution(10887771852481486698)
XLA Ops:
  0.0 150.2 %shard_map.46 = (f32[640,128]{1,0:T(8,128)}, f32[640,128]{1,0:T(8,128)}, f32[1,128]{1,0:T(1,128)}) custom-call(f32[1280,640]{1,0:T(8,128)} %green_h.1, f32[1280,128]{1,0:T(8,128)} %data_h.1, s32[3,640]{1,0:T(4,128)} %nb_h.1, f32[1,128]{1,0:T(1,128)} %bitcast.3), custom_call_target="tpu_custom_call" | custom-call | tf_op jit(solution)/shard_map/pallas_call | solution.py:621
  150.2 1.8 %multiply_add_fusion = f32[640,128]{1,0:T(8,128)} fusion(f32[640,128]{1,0:T(8,128)} %get-tuple-element.8, f32[640,128]{1,0:T(8,128)} %get-tuple-element.10, f32[128]{0:T(128)} %bitcast.2), kind=kLoop, calls=%fused_computation | loop fusion | flops 163840 | bytes 983552 | tf_op jit(solution)/shard_map/add | solution.py:630

commit v3 on v2

--- a/solution.py
+++ b/solution.py
@@ -36,14 +36,22 @@
     R = rows // 2 // nz
     BR = cols // n_obs
     half = rows // 2
-    per = 4
-    nch = n_obs // per
-    nd = rd.shape[1]
-    PD = nz // nd
+    per = nch = math.isqrt(n_obs)
     CB = cols // BAND
     Q = nz // 4
     plus = list(range(1, Q + 1))
     minus = list(range(1, Q))
+    near = [0] + [sgn * k for k in minus for sgn in (1, -1)] + [Q]
+    far = [2 * Q] + [sgn * k for k in range(2 * Q - 1, Q, -1) for sgn in (1, -1)] + [-Q]
+    pieces = near + far
+    NP = len(near)
+    quarter = half // 2
+
+    def wrapped(o):
+        return (o + 2 * Q - 1) % nz - 2 * Q + 1
+
+    def idx(o):
+        return pieces.index(wrapped(o))
     obs = lax.axis_index("obs")
     pat = lax.axis_index("patch")
     z = pat // 2
@@ -63,51 +71,77 @@
     def pair(sem, *idx):
         return sem.at[(0,) + idx], sem.at[(1,) + idx]
 
-    nblk = rows // BAND
-
-    def load(i):
-        r0 = pl.multiple_of(i * BAND, BAND)
-        return pltpu.make_async_copy(green_h.at[pl.ds(r0, BAND)], green.at[pl.ds(r0, BAND)], sem_l.at[i])
-
-    small = [pltpu.make_async_copy(src, dst, sem_l.at[nblk + i])
-             for i, (src, dst) in enumerate(((data_h, data), (nb_h, nb), (rw_h, rw)))]
-    small[0].start()
-
-    @pl.loop(0, nblk)
-    def _(i):
-        load(i).start()
-
-    for copy in small[1:]:
+    def load(n):
+        part, h, r = n // (2 * NP), n // NP % 2, n % NP
+        o = pieces[part * NP + r]
+        src = pl.multiple_of(h * half + (z + (1 - 2 * h) * o + nz) % nz * R, R)
+        return [pltpu.make_async_copy(a_.at[pl.ds(src, R)], b_.at[pl.ds(n * R, R)], sem_l.at[k, n])
+                for k, (a_, b_) in enumerate(((green_h, green), (data_h, data)))]
+
+    for n in range(2 * nz):
+        for copy in load(n):
+            copy.start()
+
+    small = [pltpu.make_async_copy(src, dst, sem_l.at[i, 2 * nz])
+             for i, (src, dst) in enumerate(((nb_h, nb), (rw_h, rw)))]
+    for copy in small:
         copy.start()
 
     barrier = pltpu.get_barrier_semaphore()
 
-    @pl.loop(1, n_patch)
-    def _(i):
-        pl.semaphore_signal(barrier, inc=1, device_id=at(obs, (pat + i) % n_patch), device_id_type=MESH)
+    def greet(o, q):
+        pl.semaphore_signal(barrier, inc=1, device_id=at(o, q), device_id_type=MESH)
+
+    greet(obs, (pat + nz) % n_patch)
+
+    @pl.loop(1, nz)
+    def _(i):
+        greet(obs, (pat + nz + i) % n_patch)
+        greet(obs, (pat + nz - i) % n_patch)
 
     @pl.loop(1, n_obs)
     def _(i):
-        pl.semaphore_signal(barrier, inc=1, device_id=at((obs + i) % n_obs, pat), device_id_type=MESH)
-
-    small[0].wait()
-
-    @pl.loop(0, nblk)
-    def _(i):
-        r0 = pl.multiple_of(i * BAND, BAND)
-        load(i).wait()
-        block = green[pl.ds(r0, BAND), :]
-        hi, lo = split(block)
-        ghi[pl.ds(r0, BAND), :] = hi
-        glo[pl.ds(r0, BAND), :] = lo
-        hi, lo = split(block.T)
-        gthi[:, pl.ds(r0, BAND)] = hi
-        gtlo[:, pl.ds(r0, BAND)] = lo
-        hi, lo = split(data[pl.ds(r0, BAND), :])
-        cat_r[pl.ds(r0, BAND), 0:E] = hi
-        cat_r[pl.ds(r0, BAND), E:2 * E] = lo
-
-    for copy in small[1:]:
+        greet((obs + i) % n_obs, pat)
+
+    def put_cat(where, value):
+        hi, lo = split(value)
+        cat_r[where, 0:E] = hi
+        cat_r[where, E:2 * E] = lo
+
+    def product(m0, m1, k0, k1):
+        y = dot(gthi[m0:m1, k0:k1], cat_r[k0:k1, :])
+        y = y[:, :E] + y[:, E:] + dot(gtlo[m0:m1, k0:k1], cat_r[k0:k1, 0:E])
+        return y.reshape((m1 - m0) // BR, BR, E)
+
+    def first_product(r0):
+        y = product(0, cols, r0, r0 + STEP)
+        if r0 == 0:
+            bs[0] = y
+        else:
+            bs[0] += y
+
+    STEP = 2 * BAND
+    loaded = 0
+    for r0 in range(0, rows, STEP):
+        while loaded * R < r0 + STEP:
+            for copy in load(loaded):
+                copy.wait()
+            loaded += 1
+        if r0:
+            first_product(r0 - STEP)
+        for r in range(r0, r0 + STEP, BAND):
+            block = green[r:r + BAND, :]
+            hi, lo = split(block)
+            ghi[r:r + BAND, :] = hi
+            glo[r:r + BAND, :] = lo
+            hi, lo = split(block.T)
+            gthi[:, r:r + BAND] = hi
+            gtlo[:, r:r + BAND] = lo
+            put_cat(slice(r, r + BAND), data[r:r + BAND, :])
+
+    first_product(rows - STEP)
+
+    for copy in small:
         copy.wait()
     weight = rw[...]
 
@@ -140,6 +174,14 @@
             lmt[pl.ds(r0, BAND), :] = m.astype(BF16)
             lm[:, pl.ds(r0, BAND)] = m.T.astype(BF16)
 
+    side = math.isqrt(n_obs)
+    steps = sorted(range(side), key=lambda k: -min(k, side - k))
+    far_first = sorted([(i, j) for i in steps for j in steps if i or j],
+                       key=lambda ij: -sum(min(k, side - k) for k in ij))
+
+    def shifted(i, j):
+        return (obs // side + i) % side * side + (obs + j) % side
+
     def bcopy(b, o, slot):
         return rcopy(bs.at[b, o], br.at[b, slot], (sem_b.at[0, b, o], sem_b.at[1, b, slot]), at(o, pat))
 
@@ -149,30 +191,33 @@
                      (sem_a.at[0, b, o], sem_a.at[1, b, slot]), at(o, pat))
 
     def backward(b, hook):
-        @pl.loop(1, nch + 1)
-        def _(j):
-            ch = (obs // per + j) % nch
-            r0 = pl.multiple_of(ch * (per * BR), per * BR)
-            y = dot(gthi[pl.ds(r0, per * BR), :], cat_r[...])
-            y = y[:, :E] + y[:, E:] + dot(gtlo[pl.ds(r0, per * BR), :], cat_r[:, 0:E])
-            bs[b, pl.ds(ch * per, per)] = y.reshape(per, BR, E)
-            if b == 0:
-                return
-            for i in range(per):
-                o = ch * per + i
-
-                @pl.when(o != obs)
-                def _():
-                    bcopy(b, o, obs).start()
-
-        hook()
-
         if b == 0:
             pl.semaphore_wait(barrier, n_patch - 1 + n_obs - 1)
 
-            @pl.loop(1, n_obs)
-            def _(i):
-                bcopy(b, (obs + i) % n_obs, obs).start()
+            for i, j in far_first:
+                bcopy(b, shifted(i, j), obs).start()
+        else:
+            for o in far:
+                if o != -Q:
+                    gwait(b - 1, o)
+                    icopy(b - 1, o).start()
+
+            for o in far:
+                icopy(b - 1, o).wait_recv()
+
+            for h in range(2):
+                put_cat(slice(half + h * quarter, half + (h + 1) * quarter), img[b - 1, h, NP:].reshape(quarter, E))
+            for i in steps:
+                ch = (obs // side + i) % side
+                r0 = pl.multiple_of(ch * (per * BR), per * BR)
+                y = dot(gthi[pl.ds(r0, per * BR), half:], cat_r[half:, :])
+                y = y[:, :E] + y[:, E:] + dot(gtlo[pl.ds(r0, per * BR), half:], cat_r[half:, 0:E])
+                bs[b, pl.ds(ch * per, per)] += y.reshape(per, BR, E)
+                for j in steps:
+                    if i or j:
+                        bcopy(b, shifted(i, j), obs).start()
+
+        hook()
 
         def add(i, acc):
             o = (obs + i) % n_obs
@@ -182,9 +227,8 @@
         total = lax.fori_loop(1, n_obs, add, bs[b, obs])
         ag[b, pl.ds(pl.multiple_of(obs * BR, BR), BR), :] = total
 
-        @pl.loop(1, n_obs)
-        def _(i):
-            acopy(b, (obs + i) % n_obs, obs).start()
+        for i, j in far_first:
+            acopy(b, shifted(i, j), obs).start()
 
         @pl.loop(1, n_obs)
         def _(i):
@@ -199,13 +243,12 @@
             acopy(b, o, obs).wait_send()
 
     def dcopy(it, k):
-        return rcopy(pf.at[pl.ds(k * PD, PD)], rd.at[it, k], pair(sem_d, it, k), at(obs, partner))
+        return rcopy(pf.at[pl.ds(k * NP, NP)], rd.at[it, k], pair(sem_d, it, k), at(obs, partner))
+
+    turn = 1 - 2 * c
 
     def zat(k):
-        return at(obs, ((z + k + nz) % nz) * 2 + c)
-
-    def owner(k):
-        return (z + k + 2 * nz) % nz
+        return at(obs, ((z + turn * k + nz) % nz) * 2 + c)
 
     first_step = ([(-k, -k - Q) for k in reversed(plus)] + [(k, k + Q) for k in reversed(minus)]
                   + [(-k, -k) for k in reversed(minus)] + [(k, k) for k in reversed(minus)])
@@ -213,26 +256,27 @@
 
     def zcopy(it, slot):
         k, o = first_step[slot]
-        return rcopy(s.at[owner(o)], zr.at[it, slot], pair(sem_z, it, slot), zat(k))
+        return rcopy(s.at[idx(o)], zr.at[it, slot], pair(sem_z, it, slot), zat(k))
 
     def fcopy(it, slot):
         return rcopy(zrel.at[slot], zfin.at[it, slot], pair(sem_f, it, slot), zat(-Q if slot == 0 else Q))
 
-    near = [(k, 0) for k in (-Q, Q) ] + [(sgn * k, 0) for k in reversed(minus) for sgn in (1, -1)]
-    relay_p = [(k, -Q) for k in reversed(plus)]
-    relay_m = [(-k, Q) for k in reversed(minus)]
-    gather = near + relay_p + relay_m
+    gather = ([(k, 0) for k in (-Q, Q)] + [(sgn * k, 0) for k in reversed(minus) for sgn in (1, -1)]
+              + [(k, -Q) for k in reversed(plus)] + [(-k, Q) for k in reversed(minus)])
+    n_own = 2 * Q
 
     def gcopy(it, m):
         k, o = gather[m]
-        p = owner(o)
-        return rcopy(img.at[it, c, p], img.at[it, c, p], (sem_g.at[0, it, m], sem_g.at[1, it, p]), zat(k))
-
-    def gwait(it, p):
-        rcopy(img.at[it, c, p], img.at[it, c, p], (sem_g.at[0, it, 0], sem_g.at[1, it, p]), zat(1)).wait_recv()
-
-    def icopy(it, k):
-        return rcopy(img.at[it, c, k], img.at[it, c, k], pair(sem_i, it, k), at(obs, partner))
+        to = idx(o - k)
+        return rcopy(img.at[it, c, idx(o)], img.at[it, c, to], (sem_g.at[0, it, m], sem_g.at[1, it, to]), zat(k))
+
+    def gwait(it, o):
+        piece = img.at[it, c, idx(o)]
+        rcopy(piece, piece, (sem_g.at[0, it, 0], sem_g.at[1, it, idx(o)]), zat(1)).wait_recv()
+
+    def icopy(it, o):
+        piece = img.at[it, c, idx(o)]
+        return rcopy(piece, piece, pair(sem_i, it, idx(o)), at(obs, partner))
 
     def fold(acc, it, slots):
         for slot in slots:
@@ -256,28 +300,28 @@
         cat_d[:, 0:E] = hi
         cat_d[:, E:2 * E] = lo
 
-        def part(h):
-            r0 = pl.multiple_of(h * half, half)
-            y = dot(ghi[pl.ds(r0, half), :], cat_d[...])
-            y = y[:, :E] + y[:, E:] + dot(glo[pl.ds(r0, half), :], cat_d[:, 0:E])
-            return y.reshape(nz, R, E)
-
-        pf[...] = part(other)
-
-        for k in range(nd):
+        def part(h, k):
+            r0 = pl.multiple_of(k * half + h * quarter, quarter)
+            y = dot(ghi[pl.ds(r0, quarter), :], cat_d[...])
+            y = y[:, :E] + y[:, E:] + dot(glo[pl.ds(r0, quarter), :], cat_d[:, 0:E])
+            return y.reshape(NP, R, E)
+
+        for k in (1, 0):
+            pf[k * NP:(k + 1) * NP] = part(other, k)
             dcopy(it, k).start()
 
         if it:
             dots(it - 1)
 
-        s[...] = part(c)
-
-        for k in range(nd):
-            dcopy(it, k).wait_recv()
-            s[k * PD:(k + 1) * PD] += rd[it, k]
-
+        for k in (1, 0):
+            s[k * NP:(k + 1) * NP] = part(c, k)
+
+        dcopy(it, 1).wait_recv()
+        s[NP:] += rd[it, 1]
         for slot in range(n_plus + n_minus):
             zcopy(it, slot).start()
+        dcopy(it, 0).wait_recv()
+        s[:NP] += rd[it, 0]
 
         if it:
             sums_mid(it - 1)
@@ -293,14 +337,14 @@
         for slot in range(n_plus + n_minus, len(first_step)):
             zcopy(it, slot).start()
 
-        zrel[0] = fold(s[owner(-Q)], it, range(n_plus))
+        zrel[0] = fold(s[idx(-Q)], it, range(n_plus))
         fcopy(it, 0).start()
-        zrel[1] = fold(s[owner(Q)], it, range(n_plus, n_plus + n_minus))
+        zrel[1] = fold(s[idx(Q)], it, range(n_plus, n_plus + n_minus))
         fcopy(it, 1).start()
 
         scalars = hook()
 
-        total = fold(s[z], it, range(n_plus + n_minus, len(first_step)))
+        total = fold(s[idx(0)], it, range(n_plus + n_minus, len(first_step)))
         for slot in range(2):
             fcopy(it, slot).wait_recv()
             total = total + zfin[it, slot]
@@ -318,40 +362,38 @@
             sq = None
             qg[...] = rest
             qd[...] = total
-            img[it, c, z] = total
-            for m in range(len(near)):
+            img[it, c, idx(0)] = total
+            for m in range(n_own):
                 gcopy(it, m).start()
-            icopy(it, z).start()
-            gwait(it, owner(-Q))
-            for m in range(len(near), len(near) + len(relay_p)):
+            icopy(it, 0).start()
+            gwait(it, -Q)
+            for m in range(n_own, n_own + Q):
                 gcopy(it, m).start()
-            gwait(it, owner(Q))
-            for m in range(len(near) + len(relay_p), len(gather)):
+            gwait(it, Q)
+            for m in range(n_own + Q, len(gather)):
                 gcopy(it, m).start()
-            icopy(it, owner(-Q)).start()
-            icopy(it, owner(Q)).start()
-            seen = {0, nz - Q, Q}
-
-            for k in minus:
-                for o in (-k, k):
-                    gwait(it, owner(o))
-                    icopy(it, owner(o)).start()
-                    seen.add(o % nz)
-            for o in range(nz):
-                if o not in seen:
-                    gwait(it, owner(o))
-                    icopy(it, owner(o)).start()
-
-            for o in range(nz):
-                icopy(it, owner(o)).wait_recv()
-            hi, lo = split(img[it].reshape(rows, E))
-            cat_r[:, 0:E] = hi
-            cat_r[:, E:2 * E] = lo
+            icopy(it, Q).start()
+            icopy(it, -Q).start()
+            for o in near[1:-1]:
+                gwait(it, o)
+                icopy(it, o).start()
+
+            for o in near:
+                icopy(it, o).wait_recv()
+            for h in range(2):
+                put_cat(slice(h * quarter, (h + 1) * quarter), img[it, h, :NP].reshape(quarter, E))
+
+            @pl.loop(0, nch)
+            def _(ch):
+                r0 = pl.multiple_of(ch * (per * BR), per * BR)
+                y = dot(gthi[pl.ds(r0, per * BR), :half], cat_r[:half, :])
+                y = y[:, :E] + y[:, E:] + dot(gtlo[pl.ds(r0, per * BR), :half], cat_r[:half, 0:E])
+                bs[it + 1, pl.ds(ch * per, per)] = y.reshape(per, BR, E)
 
         return sq
 
     def forward_end(it):
-        for k in range(nd):
+        for k in range(2):
             dcopy(it, k).wait_send()
         for slot in range(len(first_step)):
             zcopy(it, slot).wait_send()
@@ -361,9 +403,8 @@
             for m in range(len(gather)):
                 gcopy(it, m).wait_send()
 
-            @pl.loop(0, nz)
-            def _(k):
-                icopy(it, k).wait_send()
+            for o in pieces:
+                icopy(it, o).wait_send()
 
     def halo_wait(it):
         @pl.when(has_l)
@@ -464,7 +505,7 @@
     def sums_end(it):
         @pl.loop(1, nz)
         def _(k):
-            scopy(it, k, owner(k)).wait_recv()
+            scopy(it, k, (z - turn * k + nz) % nz).wait_recv()
 
         return jnp.sum(scr[it], axis=0)
 
@@ -520,11 +561,8 @@
         if it == ITERS - 1:
             laplace()
 
-            def energy(i, acc):
-                _, u = lap_rows(i)
-                return acc + jnp.sum((u * u).reshape(BAND // 8, 8, E), axis=0)
-
-            regs.append(rowsum(lax.fori_loop(0, CB, energy, jnp.zeros((8, E), F32))))
+            _, u = lap_rows(jnp.minimum(obs, CB - 1))
+            regs.append(jnp.where(obs < CB, rowsum(u * u), 0.0))
             for k, (src, dst) in enumerate(((slip, slip_h), (d, d_h))):
                 pltpu.make_async_copy(src, dst, sem_o.at[k]).start()
         return step, ratio
@@ -541,7 +579,7 @@
         reg_done(it - 1)
     last = ITERS - 1
     norm = norms[-1]
-    sq = sq + jnp.where(obs == 0, regs[0], 0.0)
+    sq = sq + regs[0]
     pls[...] = sq
     plr[pat] = sq
 
@@ -592,9 +630,9 @@
     E = data.shape[1]
     n_obs, n_patch = lax.axis_size("obs"), lax.axis_size("patch")
     nz = n_patch // 2
-    nd = 4
+    nd = 2
     R, BR, ext = rows // 2 // nz, cols // n_obs, cols + 2 * BAND
-    first, messages = 4 * (nz // 4) - 3, nz - 1
+    first = 4 * (nz // 4) - 3
     V = pltpu.VMEM
     D = pltpu.SemaphoreType.DMA
     scratch = [
@@ -612,7 +650,7 @@
         V((ITERS, 2, BAND, E), F32), V((ITERS - 1, 2, BAND, E), F32),
         V((ITERS - 1, 4, E), F32), V((ITERS - 1, 4, E), F32), V((ITERS - 1, 4, E), F32), V((ITERS - 1, nz, 4, E), F32),
         V((1, E), F32), V((n_patch, 1, E), F32), V((1, E), F32), V((n_obs, 1, E), F32),
-        D((rows // BAND + 3,)), D((2,)),
+        D((2, n_patch + 1)), D((2,)),
         D((2, ITERS, nd)), D((2, ITERS, first)), D((2, ITERS, 2)), D((2, ITERS - 1, nz)), D((2, ITERS - 1, nz)),
         D((2, ITERS, n_obs)), D((2, ITERS, n_obs)), D((2, ITERS, 2)), D((2, ITERS - 1, 2)),
         D((2, ITERS - 1)), D((2, ITERS - 1, nz)), D((2, n_patch)), D((2, n_obs)),

time: 152 us -> 146 us (0.961)
  Pallas kernels: 150 us -> 144 us
    pallas_call x1, Pallas kernels: 150 us -> 144 us  [shards(): pl.pallas_call(functools.partial(kernel, n_obs, n_patch), out_shape=[jax....]
where the time goes in v3:
time: 146 us
  Pallas kernels  144 us (99%)
  other arithmetic  1.83 us (1%)
    pallas_call x1, Pallas kernels, shards(): pl.pallas_call(functools.partial(kernel, n_obs, n_patch), out_shape=[jax....  144 us

profile of v3, /device:TPU:1, one launch (start us, length us, event | category | flops | bytes accessed | tf_op | source)
XLA Modules:
  0.0 146.0 jit_solution(3478231362544999368)
XLA Ops:
  0.0 144.2 %shard_map.46 = (f32[640,128]{1,0:T(8,128)}, f32[640,128]{1,0:T(8,128)}, f32[1,128]{1,0:T(1,128)}) custom-call(f32[1280,640]{1,0:T(8,128)} %green_h.1, f32[1280,128]{1,0:T(8,128)} %data_h.1, s32[3,640]{1,0:T(4,128)} %nb_h.1, f32[1,128]{1,0:T(1,128)} %bitcast.3), custom_call_target="tpu_custom_call" | custom-call | tf_op jit(solution)/shard_map/pallas_call | solution.py:659
  144.2 1.8 %multiply_add_fusion = f32[640,128]{1,0:T(8,128)} fusion(f32[640,128]{1,0:T(8,128)} %get-tuple-element.8, f32[640,128]{1,0:T(8,128)} %get-tuple-element.10, f32[128]{0:T(128)} %bitcast.2), kind=kLoop, calls=%fused_computation | loop fusion | flops 163840 | bytes 983552 | tf_op jit(solution)/shard_map/add | solution.py:668

commit v4 on v3

--- a/solution.py
+++ b/solution.py
@@ -29,7 +29,7 @@
            ghi, glo, gthi, gtlo, lm, lmt, cat_d, cat_r, cat_e,
            d, g, a, wext, slip, hd, hg, qd, qg,
            pf, s, rd, zr, zrel, zfin, img, bs, br, ag, hal, wr, scs, scp, scz, scr, pls, plr, qls, qlr,
-           sem_l, sem_o, sem_d, sem_z, sem_f, sem_g, sem_i, sem_b, sem_a, sem_h, sem_w, sem_c, sem_s, sem_p, sem_q):
+           sem_l, sem_o, sem_d, sem_z, sem_f, sem_g, sem_i, sem_b, sem_a, sem_h, sem_w, sem_c, sem_s, sem_p, sem_q, go):
     rows, cols = green.shape
     E = data.shape[1]
     nz = n_patch // 2
@@ -71,37 +71,63 @@
     def pair(sem, *idx):
         return sem.at[(0,) + idx], sem.at[(1,) + idx]
 
+    STEP = 2 * BAND
+    ends = [-(-(r0 + STEP) // R) for r0 in range(0, rows, STEP)]
+
     def load(n):
         part, h, r = n // (2 * NP), n // NP % 2, n % NP
         o = pieces[part * NP + r]
         src = pl.multiple_of(h * half + (z + (1 - 2 * h) * o + nz) % nz * R, R)
-        return [pltpu.make_async_copy(a_.at[pl.ds(src, R)], b_.at[pl.ds(n * R, R)], sem_l.at[k, n])
+        return [pltpu.make_async_copy(a_.at[pl.ds(src, R)], b_.at[pl.ds(n * R, R)], sem_l.at[k, sum(n >= e for e in ends)])
                 for k, (a_, b_) in enumerate(((green_h, green), (data_h, data)))]
 
+    small = [pltpu.make_async_copy(src, dst, sem_l.at[i, len(ends)])
+             for i, (src, dst) in enumerate(((nb_h, nb), (rw_h, rw)))]
+    barrier = pltpu.get_barrier_semaphore()
+
+    def greet(o, q):
+        pl.semaphore_signal(barrier, inc=1, device_id=at(o, q), device_id_type=MESH)
+
+    def tell(k):
+        pl.semaphore_signal(go.at[k], inc=1, device_id=at(obs, partner), device_id_type=MESH)
+
+    def plane_entered():
+        @pl.when(c == 0)
+        def _():
+            pl.semaphore_wait(barrier, 2 * n_obs - 1)
+            tell(0)
+
+        @pl.when(c == 1)
+        def _():
+            pl.semaphore_wait(go.at[0], 1)
+
+    def line_entered():
+        @pl.when(c == 1)
+        def _():
+            pl.semaphore_wait(barrier, n_patch - 1)
+            tell(1)
+
+        @pl.when(c == 0)
+        def _():
+            pl.semaphore_wait(go.at[1], 1)
+
     for n in range(2 * nz):
+        if n == nz // 2:
+            greet(obs, partner)
+
+            @pl.loop(1, n_obs)
+            def _(i):
+                greet((obs + i) % n_obs, z * 2)
+
+            @pl.loop(1, nz)
+            def _(k):
+                greet(obs, (z + k) % nz * 2 + 1)
+
         for copy in load(n):
             copy.start()
 
-    small = [pltpu.make_async_copy(src, dst, sem_l.at[i, 2 * nz])
-             for i, (src, dst) in enumerate(((nb_h, nb), (rw_h, rw)))]
     for copy in small:
         copy.start()
-
-    barrier = pltpu.get_barrier_semaphore()
-
-    def greet(o, q):
-        pl.semaphore_signal(barrier, inc=1, device_id=at(o, q), device_id_type=MESH)
-
-    greet(obs, (pat + nz) % n_patch)
-
-    @pl.loop(1, nz)
-    def _(i):
-        greet(obs, (pat + nz + i) % n_patch)
-        greet(obs, (pat + nz - i) % n_patch)
-
-    @pl.loop(1, n_obs)
-    def _(i):
-        greet((obs + i) % n_obs, pat)
 
     def put_cat(where, value):
         hi, lo = split(value)
@@ -120,13 +146,12 @@
         else:
             bs[0] += y
 
-    STEP = 2 * BAND
     loaded = 0
-    for r0 in range(0, rows, STEP):
-        while loaded * R < r0 + STEP:
-            for copy in load(loaded):
-                copy.wait()
-            loaded += 1
+    for n, r0 in enumerate(range(0, rows, STEP)):
+        span = pl.ds(loaded * R, (ends[n] - loaded) * R)
+        for k, (a_, b_) in enumerate(((green_h, green), (data_h, data))):
+            pltpu.make_async_copy(a_.at[span], b_.at[span], sem_l.at[k, n]).wait()
+        loaded = ends[n]
         if r0:
             first_product(r0 - STEP)
         for r in range(r0, r0 + STEP, BAND):
@@ -183,27 +208,31 @@
         return (obs // side + i) % side * side + (obs + j) % side
 
     def bcopy(b, o, slot):
-        return rcopy(bs.at[b, o], br.at[b, slot], (sem_b.at[0, b, o], sem_b.at[1, b, slot]), at(o, pat))
+        return rcopy(bs.at[b, o], br.at[b, slot], pair(sem_b, b), at(o, pat))
+
+    def ball(b):
+        return rcopy(bs.at[b, pl.ds(0, n_obs - 1)], br.at[b, pl.ds(0, n_obs - 1)], pair(sem_b, b), at(obs, partner))
 
     def acopy(b, o, slot):
-        r0 = pl.multiple_of(slot * BR, BR)
-        return rcopy(ag.at[b, pl.ds(r0, BR)], ag.at[b, pl.ds(r0, BR)],
-                     (sem_a.at[0, b, o], sem_a.at[1, b, slot]), at(o, pat))
+        piece = ag.at[b, pl.ds(pl.multiple_of(slot * BR, BR), BR)]
+        return rcopy(piece, piece, pair(sem_a, b), at(o, pat))
+
+    def aall(b):
+        block = ag.at[b, pl.ds(0, (n_obs - 1) * BR)]
+        return rcopy(block, block, pair(sem_a, b), at(obs, partner))
 
     def backward(b, hook):
         if b == 0:
-            pl.semaphore_wait(barrier, n_patch - 1 + n_obs - 1)
+            plane_entered()
 
             for i, j in far_first:
                 bcopy(b, shifted(i, j), obs).start()
         else:
-            for o in far:
-                if o != -Q:
-                    gwait(b - 1, o)
-                    icopy(b - 1, o).start()
-
-            for o in far:
-                icopy(b - 1, o).wait_recv()
+            for i in range(NP, nz - 1):
+                gall(b - 1, i, 1).wait_recv()
+                icopy(b - 1, i).start()
+
+            icopy(b - 1, NP, NP).wait_recv()
 
             for h in range(2):
                 put_cat(slice(half + h * quarter, half + (h + 1) * quarter), img[b - 1, h, NP:].reshape(quarter, E))
@@ -219,28 +248,21 @@
 
         hook()
 
-        def add(i, acc):
-            o = (obs + i) % n_obs
-            bcopy(b, o, o).wait_recv()
-            return acc + br[b, o]
-
-        total = lax.fori_loop(1, n_obs, add, bs[b, obs])
+        ball(b).wait_recv()
+        total = lax.fori_loop(1, n_obs, lambda i, acc: acc + br[b, (obs + i) % n_obs], bs[b, obs])
         ag[b, pl.ds(pl.multiple_of(obs * BR, BR), BR), :] = total
 
         for i, j in far_first:
             acopy(b, shifted(i, j), obs).start()
 
-        @pl.loop(1, n_obs)
-        def _(i):
-            o = (obs + i) % n_obs
-            acopy(b, o, o).wait_recv()
+        if b == 0:
+            line_entered()
+
+        aall(b).wait_recv()
 
     def backward_end(b):
-        @pl.loop(1, n_obs)
-        def _(i):
-            o = (obs + i) % n_obs
-            bcopy(b, o, obs).wait_send()
-            acopy(b, o, obs).wait_send()
+        ball(b).wait_send()
+        aall(b).wait_send()
 
     def dcopy(it, k):
         return rcopy(pf.at[pl.ds(k * NP, NP)], rd.at[it, k], pair(sem_d, it, k), at(obs, partner))
@@ -254,33 +276,47 @@
                   + [(-k, -k) for k in reversed(minus)] + [(k, k) for k in reversed(minus)])
     n_plus, n_minus = len(plus), len(minus)
 
+    groups = [(0, n_plus), (n_plus, n_minus), (n_plus + n_minus, len(first_step) - n_plus - n_minus)]
+
     def zcopy(it, slot):
         k, o = first_step[slot]
-        return rcopy(s.at[idx(o)], zr.at[it, slot], pair(sem_z, it, slot), zat(k))
+        group = sum(slot >= first for first, _ in groups)
+        return rcopy(s.at[idx(o)], zr.at[it, slot], (sem_z.at[it, 0], sem_z.at[it, group]), zat(k))
+
+    def zall(it, group, first, n):
+        block = zr.at[it, pl.ds(first, n)]
+        return rcopy(block, block, (sem_z.at[it, 0], sem_z.at[it, group]), at(obs, partner))
 
     def fcopy(it, slot):
-        return rcopy(zrel.at[slot], zfin.at[it, slot], pair(sem_f, it, slot), zat(-Q if slot == 0 else Q))
+        return rcopy(zrel.at[slot], zfin.at[it, slot], pair(sem_f, it), zat(-Q if slot == 0 else Q))
+
+    def fall(it):
+        return rcopy(zrel, zfin.at[it], pair(sem_f, it), at(obs, partner))
 
     gather = ([(k, 0) for k in (-Q, Q)] + [(sgn * k, 0) for k in reversed(minus) for sgn in (1, -1)]
               + [(k, -Q) for k in reversed(plus)] + [(-k, Q) for k in reversed(minus)])
     n_own = 2 * Q
 
+    def arrival(it, i):
+        return sem_g.at[it, 1 if 0 < i < NP - 1 else i - NP + 3]
+
     def gcopy(it, m):
         k, o = gather[m]
         to = idx(o - k)
-        return rcopy(img.at[it, c, idx(o)], img.at[it, c, to], (sem_g.at[0, it, m], sem_g.at[1, it, to]), zat(k))
-
-    def gwait(it, o):
-        piece = img.at[it, c, idx(o)]
-        rcopy(piece, piece, (sem_g.at[0, it, 0], sem_g.at[1, it, idx(o)]), zat(1)).wait_recv()
-
-    def icopy(it, o):
-        piece = img.at[it, c, idx(o)]
-        return rcopy(piece, piece, pair(sem_i, it, idx(o)), at(obs, partner))
-
-    def fold(acc, it, slots):
-        for slot in slots:
-            zcopy(it, slot).wait_recv()
+        return rcopy(img.at[it, c, idx(o)], img.at[it, c, to], (sem_g.at[it, 0], arrival(it, to)), zat(k))
+
+    def gall(it, i, n):
+        block = img.at[it, c, pl.ds(i, n)]
+        return rcopy(block, block, (sem_g.at[it, 0], arrival(it, i)), at(obs, partner))
+
+    def icopy(it, i, n=1):
+        block = img.at[it, c, pl.ds(i, n)]
+        return rcopy(block, block, (sem_i.at[it, 0], sem_i.at[it, 1 + i // NP]), at(obs, partner))
+
+    def fold(acc, it, group):
+        first, n = groups[group]
+        zall(it, group + 1, first, n).wait_recv()
+        for slot in range(first, first + n):
             acc = acc + zr[it, slot]
         return acc
 
@@ -337,17 +373,16 @@
         for slot in range(n_plus + n_minus, len(first_step)):
             zcopy(it, slot).start()
 
-        zrel[0] = fold(s[idx(-Q)], it, range(n_plus))
+        zrel[0] = fold(s[idx(-Q)], it, 0)
         fcopy(it, 0).start()
-        zrel[1] = fold(s[idx(Q)], it, range(n_plus, n_plus + n_minus))
+        zrel[1] = fold(s[idx(Q)], it, 1)
         fcopy(it, 1).start()
 
         scalars = hook()
 
-        total = fold(s[idx(0)], it, range(n_plus + n_minus, len(first_step)))
-        for slot in range(2):
-            fcopy(it, slot).wait_recv()
-            total = total + zfin[it, slot]
+        total = fold(s[idx(0)], it, 2)
+        fall(it).wait_recv()
+        total = total + zfin[it, 0] + zfin[it, 1]
 
         if it:
             step, ratio = scalars
@@ -366,20 +401,18 @@
             for m in range(n_own):
                 gcopy(it, m).start()
             icopy(it, 0).start()
-            gwait(it, -Q)
+            gall(it, idx(-Q), 1).wait_recv()
             for m in range(n_own, n_own + Q):
                 gcopy(it, m).start()
-            gwait(it, Q)
+            gall(it, idx(Q), 1).wait_recv()
             for m in range(n_own + Q, len(gather)):
                 gcopy(it, m).start()
-            icopy(it, Q).start()
-            icopy(it, -Q).start()
-            for o in near[1:-1]:
-                gwait(it, o)
-                icopy(it, o).start()
-
-            for o in near:
-                icopy(it, o).wait_recv()
+            icopy(it, idx(Q)).start()
+            icopy(it, idx(-Q)).start()
+            gall(it, 1, NP - 2).wait_recv()
+            icopy(it, 1, NP - 2).start()
+
+            icopy(it, 0, NP).wait_recv()
             for h in range(2):
                 put_cat(slice(h * quarter, (h + 1) * quarter), img[it, h, :NP].reshape(quarter, E))
 
@@ -395,16 +428,11 @@
     def forward_end(it):
         for k in range(2):
             dcopy(it, k).wait_send()
-        for slot in range(len(first_step)):
-            zcopy(it, slot).wait_send()
-        for slot in range(2):
-            fcopy(it, slot).wait_send()
+        zall(it, 1, 0, len(first_step)).wait_send()
+        fall(it).wait_send()
         if it < ITERS - 1:
-            for m in range(len(gather)):
-                gcopy(it, m).wait_send()
-
-            for o in pieces:
-                icopy(it, o).wait_send()
+            gall(it, 0, nz - 1).wait_send()
+            icopy(it, 0, nz).wait_send()
 
     def halo_wait(it):
         @pl.when(has_l)
@@ -491,7 +519,11 @@
         return rcopy(scs.at[it], scp.at[it], pair(sem_c, it), at(obs, partner))
 
     def scopy(it, k, slot):
-        return rcopy(scz.at[it], scr.at[it, slot], (sem_s.at[0, it, k], sem_s.at[1, it, slot]), zat(k))
+        return rcopy(scz.at[it], scr.at[it, slot], pair(sem_s, it), zat(k))
+
+    def sall(it):
+        block = scr.at[it, pl.ds(0, nz - 1)]
+        return rcopy(block, block, pair(sem_s, it), at(obs, partner))
 
     def sums_mid(it):
         ccopy(it).wait_recv()
@@ -503,24 +535,22 @@
             scopy(it, k, z).start()
 
     def sums_end(it):
-        @pl.loop(1, nz)
-        def _(k):
-            scopy(it, k, (z - turn * k + nz) % nz).wait_recv()
-
+        sall(it).wait_recv()
         return jnp.sum(scr[it], axis=0)
 
     def sums_done(it):
         ccopy(it).wait_send()
-
-        @pl.loop(1, nz)
-        def _(k):
-            scopy(it, k, z).wait_send()
+        sall(it).wait_send()
 
     def pcopy(q, slot):
-        return rcopy(pls, plr.at[slot], (sem_p.at[0, q], sem_p.at[1, slot]), at(obs, q))
-
-    def qcopy(o, slot):
-        return rcopy(qls, qlr.at[slot], (sem_q.at[0, o], sem_q.at[1, slot]), at(o, pat))
+        return rcopy(pls, plr.at[slot], pair(sem_p), at(obs, q))
+
+    def qcopy(o, core, slot):
+        return rcopy(qls, qlr.at[slot], pair(sem_q), at(o, 2 * z + core))
+
+    def rows_of(sem, n):
+        block = plr.at[pl.ds(0, n)]
+        return rcopy(block, block, pair(sem), at(obs, partner))
 
     def rowsum(x):
         return jnp.sum(x, axis=0, keepdims=True)
@@ -581,11 +611,10 @@
     norm = norms[-1]
     sq = sq + regs[0]
     pls[...] = sq
-    plr[pat] = sq
-
-    @pl.loop(1, n_patch)
-    def _(i):
-        pcopy((pat + i) % n_patch, pat).start()
+
+    @pl.loop(c, nz)
+    def _(k):
+        pcopy((z + k) % nz * 2 + 1, pat).start()
 
     forward_end(last)
     for it in range(ITERS):
@@ -593,36 +622,40 @@
     for it in range(ITERS - 1):
         sums_done(it)
 
-    @pl.loop(1, n_patch)
-    def _(i):
-        q = (pat + i) % n_patch
-        pcopy(q, q).wait_recv()
-
-    line = jnp.sum(plr[...], axis=0)
-    qls[...] = line
-    qlr[obs] = line
-
-    @pl.loop(1, n_obs)
-    def _(i):
-        qcopy((obs + i) % n_obs, obs).start()
-
-    @pl.loop(1, n_patch)
-    def _(i):
-        pcopy((pat + i) % n_patch, pat).wait_send()
+    @pl.when(c == 1)
+    def _():
+        plr[pat] = sq
+
+        rows_of(sem_p, n_patch - 1).wait_recv()
+
+    @pl.when(c == 1)
+    def _():
+        line = jnp.sum(plr[...], axis=0)
+        qls[...] = line
+        qlr[obs] = line
+        for i, j in far_first:
+            for core in range(2):
+                qcopy(shifted(i, j), core, obs).start()
+        qcopy(obs, 0, obs).start()
+
+    for core in range(2):
+        @pl.when(c == core)
+        def _():
+            rows_of(sem_p, nz - core).wait_send()
 
     for k, (src, dst) in enumerate(((slip, slip_h), (d, d_h))):
         pltpu.make_async_copy(src, dst, sem_o.at[k]).wait()
 
-    @pl.loop(1, n_obs)
-    def _(i):
-        o = (obs + i) % n_obs
-        qcopy(o, o).wait_recv()
+    for core in range(2):
+        @pl.when(c == core)
+        def _():
+            rows_of(sem_q, n_obs - core).wait_recv()
 
     scale[...] = norm / jnp.sum(qlr[...], axis=0)
 
-    @pl.loop(1, n_obs)
-    def _(i):
-        qcopy((obs + i) % n_obs, obs).wait_send()
+    @pl.when(c == 1)
+    def _():
+        rows_of(sem_q, 2 * n_obs - 1).wait_send()
 
 
 def shards(green, data, neighbours, reg_weight):
@@ -650,10 +683,10 @@
         V((ITERS, 2, BAND, E), F32), V((ITERS - 1, 2, BAND, E), F32),
         V((ITERS - 1, 4, E), F32), V((ITERS - 1, 4, E), F32), V((ITERS - 1, 4, E), F32), V((ITERS - 1, nz, 4, E), F32),
         V((1, E), F32), V((n_patch, 1, E), F32), V((1, E), F32), V((n_obs, 1, E), F32),
-        D((2, n_patch + 1)), D((2,)),
-        D((2, ITERS, nd)), D((2, ITERS, first)), D((2, ITERS, 2)), D((2, ITERS - 1, nz)), D((2, ITERS - 1, nz)),
-        D((2, ITERS, n_obs)), D((2, ITERS, n_obs)), D((2, ITERS, 2)), D((2, ITERS - 1, 2)),
-        D((2, ITERS - 1)), D((2, ITERS - 1, nz)), D((2, n_patch)), D((2, n_obs)),
+        D((2, rows // (2 * BAND) + 1)), D((2,)),
+        D((2, ITERS, nd)), D((ITERS, 4)), D((2, ITERS)), D((ITERS - 1, nz - nz // 2 + 3)), D((ITERS - 1, 3)),
+        D((2, ITERS)), D((2, ITERS)), D((2, ITERS, 2)), D((2, ITERS - 1, 2)),
+        D((2, ITERS - 1)), D((2, ITERS - 1)), D((2,)), D((2,)), pltpu.SemaphoreType.REGULAR((2,)),
     ]
     anywhere = pl.BlockSpec(memory_space=pl.ANY)
     slip, d, scale = pl.pallas_call(

time: 146 us -> 139 us (0.952)
  Pallas kernels: 144 us -> 137 us
    pallas_call x1, Pallas kernels: 144 us -> 137 us  [shards(): pl.pallas_call(functools.partial(kernel, n_obs, n_patch), out_shape=[jax....]
where the time goes in v4:
time: 139 us
  Pallas kernels  137 us (99%)
  other arithmetic  1.83 us (1%)
    pallas_call x1, Pallas kernels, shards(): pl.pallas_call(functools.partial(kernel, n_obs, n_patch), out_shape=[jax....  137 us

profile of v4, /device:TPU:1, one launch (start us, length us, event | category | flops | bytes accessed | tf_op | source)
XLA Modules:
  0.0 138.6 jit_solution(10810528179364651314)
XLA Ops:
  0.0 136.7 %shard_map.46 = (f32[640,128]{1,0:T(8,128)}, f32[640,128]{1,0:T(8,128)}, f32[1,128]{1,0:T(1,128)}) custom-call(f32[1280,640]{1,0:T(8,128)} %green_h.1, f32[1280,128]{1,0:T(8,128)} %data_h.1, s32[3,640]{1,0:T(4,128)} %nb_h.1, f32[1,128]{1,0:T(1,128)} %bitcast.3), custom_call_target="tpu_custom_call" | custom-call | tf_op jit(solution)/shard_map/pallas_call | solution.py:692
  136.7 1.8 %multiply_add_fusion = f32[640,128]{1,0:T(8,128)} fusion(f32[640,128]{1,0:T(8,128)} %get-tuple-element.8, f32[640,128]{1,0:T(8,128)} %get-tuple-element.10, f32[128]{0:T(128)} %bitcast.2), kind=kLoop, calls=%fused_computation | loop fusion | flops 163840 | bytes 983552 | tf_op jit(solution)/shard_map/add | solution.py:701

commit v5 on v4

--- a/solution.py
+++ b/solution.py
@@ -28,8 +28,8 @@
            green, data, nb, rw,
            ghi, glo, gthi, gtlo, lm, lmt, cat_d, cat_r, cat_e,
            d, g, a, wext, slip, hd, hg, qd, qg,
-           pf, s, rd, zr, zrel, zfin, img, bs, br, ag, hal, wr, scs, scp, scz, scr, pls, plr, qls, qlr,
-           sem_l, sem_o, sem_d, sem_z, sem_f, sem_g, sem_i, sem_b, sem_a, sem_h, sem_w, sem_c, sem_s, sem_p, sem_q, go):
+           pf, s, rd, zr, zrel, zfin, img, bs, br, ag, hal, wr, scs, scp, scz, scr, tots, pls, plr, qls, qlr,
+           sem_l, sem_o, sem_d, sem_z, sem_f, sem_g, sem_i, sem_b, sem_a, sem_h, sem_w, sem_c, sem_s, sem_t, sem_p, sem_q, go):
     rows, cols = green.shape
     E = data.shape[1]
     nz = n_patch // 2
@@ -362,21 +362,34 @@
         if it:
             sums_mid(it - 1)
 
-        @pl.when(has_r)
-        def _():
-            hcopy_r(it).start()
-
-        @pl.when(has_l)
-        def _():
-            hcopy_l(it).start()
-
-        for slot in range(n_plus + n_minus, len(first_step)):
-            zcopy(it, slot).start()
+        def halos():
+            @pl.when(has_r)
+            def _():
+                hcopy_r(it).start()
+
+            @pl.when(has_l)
+            def _():
+                hcopy_l(it).start()
+
+        if last:
+            halos()
+
+        direct = range(n_plus + n_minus, len(first_step))
+        for slot in direct:
+            if abs(first_step[slot][0]) > 1:
+                zcopy(it, slot).start()
 
         zrel[0] = fold(s[idx(-Q)], it, 0)
         fcopy(it, 0).start()
         zrel[1] = fold(s[idx(Q)], it, 1)
         fcopy(it, 1).start()
+
+        for slot in direct:
+            if abs(first_step[slot][0]) == 1:
+                zcopy(it, slot).start()
+
+        if not last:
+            halos()
 
         scalars = hook()
 
@@ -401,6 +414,7 @@
             for m in range(n_own):
                 gcopy(it, m).start()
             icopy(it, 0).start()
+            halo_update(it, scalars)
             gall(it, idx(-Q), 1).wait_recv()
             for m in range(n_own, n_own + Q):
                 gcopy(it, m).start()
@@ -525,22 +539,43 @@
         block = scr.at[it, pl.ds(0, nz - 1)]
         return rcopy(block, block, pair(sem_s, it), at(obs, partner))
 
+    def tcopy(it):
+        return rcopy(tots.at[it], tots.at[it], pair(sem_t, it), at(obs, partner))
+
     def sums_mid(it):
-        ccopy(it).wait_recv()
-        scz[it] = scs[it] + scp[it]
-        scr[it, z] = scs[it] + scp[it]
-
-        @pl.loop(1, nz)
-        def _(k):
-            scopy(it, k, z).start()
+        @pl.when(c == 1)
+        def _():
+            ccopy(it).wait_recv()
+            both = scs[it] + scp[it]
+            scz[it] = both
+            scr[it, z] = both
+
+            @pl.loop(1, nz)
+            def _(k):
+                scopy(it, k, z).start()
 
     def sums_end(it):
-        sall(it).wait_recv()
-        return jnp.sum(scr[it], axis=0)
+        @pl.when(c == 1)
+        def _():
+            sall(it).wait_recv()
+            tots[it] = jnp.sum(scr[it], axis=0)
+            tcopy(it).start()
+
+        @pl.when(c == 0)
+        def _():
+            tcopy(it).wait_recv()
+
+        return tots[it]
 
     def sums_done(it):
-        ccopy(it).wait_send()
-        sall(it).wait_send()
+        @pl.when(c == 0)
+        def _():
+            ccopy(it).wait_send()
+
+        @pl.when(c == 1)
+        def _():
+            sall(it).wait_send()
+            tcopy(it).wait_send()
 
     def pcopy(q, slot):
         return rcopy(pls, plr.at[slot], pair(sem_p), at(obs, q))
@@ -563,12 +598,22 @@
         scs[it, 1:2, :] = rowsum(dv * av)
         scs[it, 2:3, :] = rowsum(gv * av)
         scs[it, 3:4, :] = rowsum(av * av)
-        ccopy(it).start()
+        @pl.when(c == 0)
+        def _():
+            ccopy(it).start()
 
     def first():
-        halo_wait(0)
-        hg[...] = hal[0]
-        hd[...] = hal[0]
+        return None
+
+    def halo_update(it, scalars):
+        halo_wait(it)
+        if it == 0:
+            hg[...] = hal[0]
+            hd[...] = hal[0]
+        else:
+            step, ratio = scalars
+            hg[...] = hg[...] - step * hal[it]
+            hd[...] = hg[...] + ratio * hd[...]
 
     def advance(it):
         tot = sums_end(it - 1)
@@ -579,16 +624,14 @@
         after = norm - 2.0 * step * tot[2:3] + step * step * tot[3:4]
         ratio = after / norm
         norms.append(after)
-        halo_wait(it)
         if it == 1:
             slip[...] = step * d[...]
         else:
             slip[...] += step * d[...]
         g[...] = g[...] - step * a[...]
         d[...] = g[...] + ratio * d[...]
-        hg[...] = hg[...] - step * hal[it]
-        hd[...] = hg[...] + ratio * hd[...]
         if it == ITERS - 1:
+            halo_update(it, (step, ratio))
             laplace()
 
             _, u = lap_rows(jnp.minimum(obs, CB - 1))
@@ -681,12 +724,12 @@
         V((ITERS - 1, 2, nz, R, E), F32),
         V((ITERS, n_obs, BR, E), F32), V((ITERS, n_obs, BR, E), F32), V((ITERS, cols, E), F32),
         V((ITERS, 2, BAND, E), F32), V((ITERS - 1, 2, BAND, E), F32),
-        V((ITERS - 1, 4, E), F32), V((ITERS - 1, 4, E), F32), V((ITERS - 1, 4, E), F32), V((ITERS - 1, nz, 4, E), F32),
+        V((ITERS - 1, 4, E), F32), V((ITERS - 1, 4, E), F32), V((ITERS - 1, 4, E), F32), V((ITERS - 1, nz, 4, E), F32), V((ITERS - 1, 4, E), F32),
         V((1, E), F32), V((n_patch, 1, E), F32), V((1, E), F32), V((n_obs, 1, E), F32),
         D((2, rows // (2 * BAND) + 1)), D((2,)),
         D((2, ITERS, nd)), D((ITERS, 4)), D((2, ITERS)), D((ITERS - 1, nz - nz // 2 + 3)), D((ITERS - 1, 3)),
         D((2, ITERS)), D((2, ITERS)), D((2, ITERS, 2)), D((2, ITERS - 1, 2)),
-        D((2, ITERS - 1)), D((2, ITERS - 1)), D((2,)), D((2,)), pltpu.SemaphoreType.REGULAR((2,)),
+        D((2, ITERS - 1)), D((2, ITERS - 1)), D((2, ITERS - 1)), D((2,)), D((2,)), pltpu.SemaphoreType.REGULAR((2,)),
     ]
     anywhere = pl.BlockSpec(memory_space=pl.ANY)
     slip, d, scale = pl.pallas_call(

time: 139 us -> 136 us (0.978)
  Pallas kernels: 137 us -> 134 us
    pallas_call x1, Pallas kernels: 137 us -> 134 us  [shards(): pl.pallas_call(functools.partial(kernel, n_obs, n_patch), out_shape=[jax....]
where the time goes in v5:
time: 136 us
  Pallas kernels  134 us (99%)
  other arithmetic  1.83 us (1%)
    pallas_call x1, Pallas kernels, shards(): pl.pallas_call(functools.partial(kernel, n_obs, n_patch), out_shape=[jax....  134 us

profile of v5, /device:TPU:1, one launch (start us, length us, event | category | flops | bytes accessed | tf_op | source)
XLA Modules:
  0.0 135.9 jit_solution(3584543051541161319)
XLA Ops:
  0.0 134.0 %shard_map.46 = (f32[640,128]{1,0:T(8,128)}, f32[640,128]{1,0:T(8,128)}, f32[1,128]{1,0:T(1,128)}) custom-call(f32[1280,640]{1,0:T(8,128)} %green_h.1, f32[1280,128]{1,0:T(8,128)} %data_h.1, s32[3,640]{1,0:T(4,128)} %nb_h.1, f32[1,128]{1,0:T(1,128)} %bitcast.3), custom_call_target="tpu_custom_call" | custom-call | tf_op jit(solution)/shard_map/pallas_call | solution.py:735
  134.0 1.8 %multiply_add_fusion = f32[640,128]{1,0:T(8,128)} fusion(f32[640,128]{1,0:T(8,128)} %get-tuple-element.8, f32[640,128]{1,0:T(8,128)} %get-tuple-element.10, f32[128]{0:T(128)} %bitcast.2), kind=kLoop, calls=%fused_computation | loop fusion | flops 163840 | bytes 983552 | tf_op jit(solution)/shard_map/add | solution.py:744

commit v6 on v5

--- a/solution.py
+++ b/solution.py
@@ -246,6 +246,8 @@
                     if i or j:
                         bcopy(b, shifted(i, j), obs).start()
 
+        if b:
+            updates.pop()()
         hook()
 
         ball(b).wait_recv()
@@ -272,7 +274,8 @@
     def zat(k):
         return at(obs, ((z + turn * k + nz) % nz) * 2 + c)
 
-    first_step = ([(-k, -k - Q) for k in reversed(plus)] + [(k, k + Q) for k in reversed(minus)]
+    W = Q + 1
+    first_step = ([(-k, -k - W) for k in reversed(minus)] + [(1, -Q)] + [(k, k + W) for k in reversed(minus[:-1])] + [(-1, Q)]
                   + [(-k, -k) for k in reversed(minus)] + [(k, k) for k in reversed(minus)])
     n_plus, n_minus = len(plus), len(minus)
 
@@ -288,7 +291,7 @@
         return rcopy(block, block, (sem_z.at[it, 0], sem_z.at[it, group]), at(obs, partner))
 
     def fcopy(it, slot):
-        return rcopy(zrel.at[slot], zfin.at[it, slot], pair(sem_f, it), zat(-Q if slot == 0 else Q))
+        return rcopy(zrel.at[slot], zfin.at[it, slot], pair(sem_f, it), zat(-W if slot == 0 else W))
 
     def fall(it):
         return rcopy(zrel, zfin.at[it], pair(sem_f, it), at(obs, partner))
@@ -354,10 +357,11 @@
 
         dcopy(it, 1).wait_recv()
         s[NP:] += rd[it, 1]
-        for slot in range(n_plus + n_minus):
+        for slot in range(n_plus + n_minus - 1):
             zcopy(it, slot).start()
         dcopy(it, 0).wait_recv()
         s[:NP] += rd[it, 0]
+        zcopy(it, n_plus + n_minus - 1).start()
 
         if it:
             sums_mid(it - 1)
@@ -379,17 +383,15 @@
             if abs(first_step[slot][0]) > 1:
                 zcopy(it, slot).start()
 
-        zrel[0] = fold(s[idx(-Q)], it, 0)
+        zrel[0] = fold(s[idx(-W)], it, 0)
         fcopy(it, 0).start()
-        zrel[1] = fold(s[idx(Q)], it, 1)
+        zrel[1] = fold(s[idx(W)], it, 1)
         fcopy(it, 1).start()
 
         for slot in direct:
             if abs(first_step[slot][0]) == 1:
                 zcopy(it, slot).start()
 
-        if not last:
-            halos()
 
         scalars = hook()
 
@@ -414,13 +416,13 @@
             for m in range(n_own):
                 gcopy(it, m).start()
             icopy(it, 0).start()
-            halo_update(it, scalars)
             gall(it, idx(-Q), 1).wait_recv()
             for m in range(n_own, n_own + Q):
                 gcopy(it, m).start()
             gall(it, idx(Q), 1).wait_recv()
             for m in range(n_own + Q, len(gather)):
                 gcopy(it, m).start()
+            halos()
             icopy(it, idx(Q)).start()
             icopy(it, idx(-Q)).start()
             gall(it, 1, NP - 2).wait_recv()
@@ -436,6 +438,8 @@
                 y = dot(gthi[pl.ds(r0, per * BR), :half], cat_r[:half, :])
                 y = y[:, :E] + y[:, E:] + dot(gtlo[pl.ds(r0, per * BR), :half], cat_r[:half, 0:E])
                 bs[it + 1, pl.ds(ch * per, per)] = y.reshape(per, BR, E)
+
+            updates.append(functools.partial(halo_update, it, scalars))
 
         return sq
 
@@ -591,6 +595,7 @@
         return jnp.sum(x, axis=0, keepdims=True)
 
     norms, regs = [], []
+    updates = []
 
     def dots(it):
         gv, dv, av = g[...], d[...], a[...]

time: 136 us -> 136 us (level)
  no operation moved by 1% of the time
where the time goes in v6:
time: 136 us
  Pallas kernels  134 us (99%)
  other arithmetic  1.83 us (1%)
    pallas_call x1, Pallas kernels, shards(): pl.pallas_call(functools.partial(kernel, n_obs, n_patch), out_shape=[jax....  134 us

profile of v6, /device:TPU:1, one launch (start us, length us, event | category | flops | bytes accessed | tf_op | source)
XLA Modules:
  0.0 135.8 jit_solution(13423389713074706197)
XLA Ops:
  0.0 134.0 %shard_map.46 = (f32[640,128]{1,0:T(8,128)}, f32[640,128]{1,0:T(8,128)}, f32[1,128]{1,0:T(1,128)}) custom-call(f32[1280,640]{1,0:T(8,128)} %green_h.1, f32[1280,128]{1,0:T(8,128)} %data_h.1, s32[3,640]{1,0:T(4,128)} %nb_h.1, f32[1,128]{1,0:T(1,128)} %bitcast.3), custom_call_target="tpu_custom_call" | custom-call | tf_op jit(solution)/shard_map/pallas_call | solution.py:740
  134.0 1.8 %multiply_add_fusion = f32[640,128]{1,0:T(8,128)} fusion(f32[640,128]{1,0:T(8,128)} %get-tuple-element.8, f32[640,128]{1,0:T(8,128)} %get-tuple-element.10, f32[128]{0:T(128)} %bitcast.2), kind=kLoop, calls=%fused_computation | loop fusion | flops 163840 | bytes 983552 | tf_op jit(solution)/shard_map/add | solution.py:749

commit v7 on v6

--- a/solution.py
+++ b/solution.py
@@ -25,7 +25,7 @@
 
 
 def kernel(n_obs, n_patch, green_h, data_h, nb_h, rw_h, slip_h, d_h, scale,
-           green, data, nb, rw,
+           green, data, line_up, nb, rw,
            ghi, glo, gthi, gtlo, lm, lmt, cat_d, cat_r, cat_e,
            d, g, a, wext, slip, hd, hg, qd, qg,
            pf, s, rd, zr, zrel, zfin, img, bs, br, ag, hal, wr, scs, scp, scz, scr, tots, pls, plr, qls, qlr,
@@ -78,11 +78,12 @@
         part, h, r = n // (2 * NP), n // NP % 2, n % NP
         o = pieces[part * NP + r]
         src = pl.multiple_of(h * half + (z + (1 - 2 * h) * o + nz) % nz * R, R)
-        return [pltpu.make_async_copy(a_.at[pl.ds(src, R)], b_.at[pl.ds(n * R, R)], sem_l.at[k, sum(n >= e for e in ends)])
-                for k, (a_, b_) in enumerate(((green_h, green), (data_h, data)))]
+        return src, pltpu.make_async_copy(green_h.at[pl.ds(src, R)], green.at[pl.ds(n * R, R)],
+                                          sem_l.at[0, sum(n >= e for e in ends)])
 
     small = [pltpu.make_async_copy(src, dst, sem_l.at[i, len(ends)])
              for i, (src, dst) in enumerate(((nb_h, nb), (rw_h, rw)))]
+    fields = pltpu.make_async_copy(data_h, data, sem_l.at[1, 0])
     barrier = pltpu.get_barrier_semaphore()
 
     def greet(o, q):
@@ -112,22 +113,22 @@
             pl.semaphore_wait(go.at[1], 1)
 
     for n in range(2 * nz):
-        if n == nz // 2:
-            greet(obs, partner)
-
-            @pl.loop(1, n_obs)
-            def _(i):
-                greet((obs + i) % n_obs, z * 2)
-
-            @pl.loop(1, nz)
-            def _(k):
-                greet(obs, (z + k) % nz * 2 + 1)
-
-        for copy in load(n):
-            copy.start()
+        load(n)[1].start()
+        if n == nz // 4:
+            fields.start()
 
     for copy in small:
         copy.start()
+
+    greet(obs, partner)
+
+    @pl.loop(1, n_obs)
+    def _(i):
+        greet((obs + i) % n_obs, z * 2)
+
+    @pl.loop(1, nz)
+    def _(k):
+        greet(obs, (z + k) % nz * 2 + 1)
 
     def put_cat(where, value):
         hi, lo = split(value)
@@ -149,8 +150,11 @@
     loaded = 0
     for n, r0 in enumerate(range(0, rows, STEP)):
         span = pl.ds(loaded * R, (ends[n] - loaded) * R)
-        for k, (a_, b_) in enumerate(((green_h, green), (data_h, data))):
-            pltpu.make_async_copy(a_.at[span], b_.at[span], sem_l.at[k, n]).wait()
+        pltpu.make_async_copy(green_h.at[span], green.at[span], sem_l.at[0, n]).wait()
+        if n == 0:
+            fields.wait()
+        for m in range(loaded, ends[n]):
+            line_up[m * R:(m + 1) * R, :] = data[pl.ds(load(m)[0], R), :]
         loaded = ends[n]
         if r0:
             first_product(r0 - STEP)
@@ -162,7 +166,7 @@
             hi, lo = split(block.T)
             gthi[:, r:r + BAND] = hi
             gtlo[:, r:r + BAND] = lo
-            put_cat(slice(r, r + BAND), data[r:r + BAND, :])
+            put_cat(slice(r, r + BAND), line_up[r:r + BAND, :])
 
     first_product(rows - STEP)
 
@@ -205,28 +209,31 @@
                        key=lambda ij: -sum(min(k, side - k) for k in ij))
 
     def shifted(i, j):
-        return (obs // side + i) % side * side + (obs + j) % side
+        return (obs // side + (1 - 2 * c) * i + side) % side * side + (obs + (1 - 2 * c) * j + side) % side
+
+    def crossed(i, j):
+        return shifted(i + c * (j - i), j + c * (i - j))
 
     def bcopy(b, o, slot):
-        return rcopy(bs.at[b, o], br.at[b, slot], pair(sem_b, b), at(o, pat))
+        return rcopy(bs.at[b, o], br.at[b, slot], pair(sem_b), at(o, pat))
 
     def ball(b):
-        return rcopy(bs.at[b, pl.ds(0, n_obs - 1)], br.at[b, pl.ds(0, n_obs - 1)], pair(sem_b, b), at(obs, partner))
+        return rcopy(bs.at[b, pl.ds(0, n_obs - 1)], br.at[b, pl.ds(0, n_obs - 1)], pair(sem_b), at(obs, partner))
 
     def acopy(b, o, slot):
         piece = ag.at[b, pl.ds(pl.multiple_of(slot * BR, BR), BR)]
-        return rcopy(piece, piece, pair(sem_a, b), at(o, pat))
+        return rcopy(piece, piece, pair(sem_a), at(o, pat))
 
     def aall(b):
         block = ag.at[b, pl.ds(0, (n_obs - 1) * BR)]
-        return rcopy(block, block, pair(sem_a, b), at(obs, partner))
+        return rcopy(block, block, pair(sem_a), at(obs, partner))
 
     def backward(b, hook):
         if b == 0:
             plane_entered()
 
             for i, j in far_first:
-                bcopy(b, shifted(i, j), obs).start()
+                bcopy(b, crossed(i, j), obs).start()
         else:
             for i in range(NP, nz - 1):
                 gall(b - 1, i, 1).wait_recv()
@@ -237,7 +244,7 @@
             for h in range(2):
                 put_cat(slice(half + h * quarter, half + (h + 1) * quarter), img[b - 1, h, NP:].reshape(quarter, E))
             for i in steps:
-                ch = (obs // side + i) % side
+                ch = (obs // side + (1 - 2 * c) * i + side) % side
                 r0 = pl.multiple_of(ch * (per * BR), per * BR)
                 y = dot(gthi[pl.ds(r0, per * BR), half:], cat_r[half:, :])
                 y = y[:, :E] + y[:, E:] + dot(gtlo[pl.ds(r0, per * BR), half:], cat_r[half:, 0:E])
@@ -255,7 +262,7 @@
         ag[b, pl.ds(pl.multiple_of(obs * BR, BR), BR), :] = total
 
         for i, j in far_first:
-            acopy(b, shifted(i, j), obs).start()
+            acopy(b, crossed(i, j), obs).start()
 
         if b == 0:
             line_entered()
@@ -267,7 +274,7 @@
         aall(b).wait_send()
 
     def dcopy(it, k):
-        return rcopy(pf.at[pl.ds(k * NP, NP)], rd.at[it, k], pair(sem_d, it, k), at(obs, partner))
+        return rcopy(pf.at[pl.ds(k * NP, NP)], rd.at[it, k], pair(sem_d, k), at(obs, partner))
 
     turn = 1 - 2 * c
 
@@ -284,37 +291,37 @@
     def zcopy(it, slot):
         k, o = first_step[slot]
         group = sum(slot >= first for first, _ in groups)
-        return rcopy(s.at[idx(o)], zr.at[it, slot], (sem_z.at[it, 0], sem_z.at[it, group]), zat(k))
+        return rcopy(s.at[idx(o)], zr.at[it, slot], (sem_z.at[0], sem_z.at[group]), zat(k))
 
     def zall(it, group, first, n):
         block = zr.at[it, pl.ds(first, n)]
-        return rcopy(block, block, (sem_z.at[it, 0], sem_z.at[it, group]), at(obs, partner))
+        return rcopy(block, block, (sem_z.at[0], sem_z.at[group]), at(obs, partner))
 
     def fcopy(it, slot):
-        return rcopy(zrel.at[slot], zfin.at[it, slot], pair(sem_f, it), zat(-W if slot == 0 else W))
+        return rcopy(zrel.at[slot], zfin.at[it, slot], pair(sem_f), zat(-W if slot == 0 else W))
 
     def fall(it):
-        return rcopy(zrel, zfin.at[it], pair(sem_f, it), at(obs, partner))
+        return rcopy(zrel, zfin.at[it], pair(sem_f), at(obs, partner))
 
     gather = ([(k, 0) for k in (-Q, Q)] + [(sgn * k, 0) for k in reversed(minus) for sgn in (1, -1)]
               + [(k, -Q) for k in reversed(plus)] + [(-k, Q) for k in reversed(minus)])
     n_own = 2 * Q
 
     def arrival(it, i):
-        return sem_g.at[it, 1 if 0 < i < NP - 1 else i - NP + 3]
+        return sem_g.at[1 if 0 < i < NP - 1 else i - NP + 3]
 
     def gcopy(it, m):
         k, o = gather[m]
         to = idx(o - k)
-        return rcopy(img.at[it, c, idx(o)], img.at[it, c, to], (sem_g.at[it, 0], arrival(it, to)), zat(k))
+        return rcopy(img.at[it, c, idx(o)], img.at[it, c, to], (sem_g.at[0], arrival(it, to)), zat(k))
 
     def gall(it, i, n):
         block = img.at[it, c, pl.ds(i, n)]
-        return rcopy(block, block, (sem_g.at[it, 0], arrival(it, i)), at(obs, partner))
+        return rcopy(block, block, (sem_g.at[0], arrival(it, i)), at(obs, partner))
 
     def icopy(it, i, n=1):
         block = img.at[it, c, pl.ds(i, n)]
-        return rcopy(block, block, (sem_i.at[it, 0], sem_i.at[it, 1 + i // NP]), at(obs, partner))
+        return rcopy(block, block, (sem_i.at[0], sem_i.at[1 + i // NP]), at(obs, partner))
 
     def fold(acc, it, group):
         first, n = groups[group]
@@ -650,6 +657,7 @@
     d[...] = ag[0]
     forward(0, first)
     for it in range(1, ITERS):
+        backward_end(it - 1)
         backward(it, functools.partial(reg_start, it - 1))
         forward_end(it - 1)
         reg_end(it - 1)
@@ -665,8 +673,7 @@
         pcopy((z + k) % nz * 2 + 1, pat).start()
 
     forward_end(last)
-    for it in range(ITERS):
-        backward_end(it)
+    backward_end(last)
     for it in range(ITERS - 1):
         sums_done(it)
 
@@ -717,7 +724,7 @@
     V = pltpu.VMEM
     D = pltpu.SemaphoreType.DMA
     scratch = [
-        V((rows, cols), F32), V((rows, E), F32), V(neighbours.shape, jnp.int32), V((1, E), F32),
+        V((rows, cols), F32), V((rows, E), F32), V((rows, E), F32), V(neighbours.shape, jnp.int32), V((1, E), F32),
         V((rows, cols), BF16), V((rows, cols), BF16),
         V((cols, rows), BF16), V((cols, rows), BF16),
         V((cols, ext), BF16), V((ext, cols), BF16),
@@ -732,8 +739,8 @@
         V((ITERS - 1, 4, E), F32), V((ITERS - 1, 4, E), F32), V((ITERS - 1, 4, E), F32), V((ITERS - 1, nz, 4, E), F32), V((ITERS - 1, 4, E), F32),
         V((1, E), F32), V((n_patch, 1, E), F32), V((1, E), F32), V((n_obs, 1, E), F32),
         D((2, rows // (2 * BAND) + 1)), D((2,)),
-        D((2, ITERS, nd)), D((ITERS, 4)), D((2, ITERS)), D((ITERS - 1, nz - nz // 2 + 3)), D((ITERS - 1, 3)),
-        D((2, ITERS)), D((2, ITERS)), D((2, ITERS, 2)), D((2, ITERS - 1, 2)),
+        D((2, nd)), D((4,)), D((2,)), D((nz - nz // 2 + 3,)), D((3,)),
+        D((2,)), D((2,)), D((2, ITERS, 2)), D((2, ITERS - 1, 2)),
         D((2, ITERS - 1)), D((2, ITERS - 1)), D((2, ITERS - 1)), D((2,)), D((2,)), pltpu.SemaphoreType.REGULAR((2,)),
     ]
     anywhere = pl.BlockSpec(memory_space=pl.ANY)

time: 136 us -> 136 us (level)
  no operation moved by 1% of the time
where the time goes in v7:
time: 136 us
  Pallas kernels  134 us (99%)
  other arithmetic  1.83 us (1%)
    pallas_call x1, Pallas kernels, shards(): pl.pallas_call(functools.partial(kernel, n_obs, n_patch), out_shape=[jax....  134 us

profile of v7, /device:TPU:1, one launch (start us, length us, event | category | flops | bytes accessed | tf_op | source)
XLA Modules:
  0.0 135.6 jit_solution(1705460916783532774)
XLA Ops:
  0.0 133.8 %shard_map.46 = (f32[640,128]{1,0:T(8,128)}, f32[640,128]{1,0:T(8,128)}, f32[1,128]{1,0:T(1,128)}) custom-call(f32[1280,640]{1,0:T(8,128)} %green_h.1, f32[1280,128]{1,0:T(8,128)} %data_h.1, s32[3,640]{1,0:T(4,128)} %nb_h.1, f32[1,128]{1,0:T(1,128)} %bitcast.3), custom_call_target="tpu_custom_call" | custom-call | tf_op jit(solution)/shard_map/pallas_call | solution.py:747
  133.8 1.8 %multiply_add_fusion = f32[640,128]{1,0:T(8,128)} fusion(f32[640,128]{1,0:T(8,128)} %get-tuple-element.8, f32[640,128]{1,0:T(8,128)} %get-tuple-element.10, f32[128]{0:T(128)} %bitcast.2), kind=kLoop, calls=%fused_computation | loop fusion | flops 163840 | bytes 983552 | tf_op jit(solution)/shard_map/add | solution.py:756

commit v8 on v7

--- a/solution.py
+++ b/solution.py
@@ -390,10 +390,10 @@
             if abs(first_step[slot][0]) > 1:
                 zcopy(it, slot).start()
 
+        zrel[1] = fold(s[idx(W)], it, 1)
+        fcopy(it, 1).start()
         zrel[0] = fold(s[idx(-W)], it, 0)
         fcopy(it, 0).start()
-        zrel[1] = fold(s[idx(W)], it, 1)
-        fcopy(it, 1).start()
 
         for slot in direct:
             if abs(first_step[slot][0]) == 1:
@@ -668,9 +668,9 @@
     sq = sq + regs[0]
     pls[...] = sq
 
-    @pl.loop(c, nz)
+    @pl.loop(0, nz - c)
     def _(k):
-        pcopy((z + k) % nz * 2 + 1, pat).start()
+        pcopy((z + (nz // 2 + k + c * (k // (nz // 2))) % nz) % nz * 2 + 1, pat).start()
 
     forward_end(last)
     backward_end(last)

time: 136 us -> 135 us (level)
  no operation moved by 1% of the time
where the time goes in v8:
time: 135 us
  Pallas kernels  133 us (99%)
  other arithmetic  1.83 us (1%)
    pallas_call x1, Pallas kernels, shards(): pl.pallas_call(functools.partial(kernel, n_obs, n_patch), out_shape=[jax....  133 us

profile of v8, /device:TPU:1, one launch (start us, length us, event | category | flops | bytes accessed | tf_op | source)
XLA Modules:
  0.0 135.1 jit_solution(2536132985542220519)
XLA Ops:
  0.0 133.3 %shard_map.46 = (f32[640,128]{1,0:T(8,128)}, f32[640,128]{1,0:T(8,128)}, f32[1,128]{1,0:T(1,128)}) custom-call(f32[1280,640]{1,0:T(8,128)} %green_h.1, f32[1280,128]{1,0:T(8,128)} %data_h.1, s32[3,640]{1,0:T(4,128)} %nb_h.1, f32[1,128]{1,0:T(1,128)} %bitcast.3), custom_call_target="tpu_custom_call" | custom-call | tf_op jit(solution)/shard_map/pallas_call | solution.py:747
  133.3 1.8 %multiply_add_fusion = f32[640,128]{1,0:T(8,128)} fusion(f32[640,128]{1,0:T(8,128)} %get-tuple-element.8, f32[640,128]{1,0:T(8,128)} %get-tuple-element.10, f32[128]{0:T(128)} %bitcast.2), kind=kLoop, calls=%fused_computation | loop fusion | flops 163840 | bytes 983552 | tf_op jit(solution)/shard_map/add | solution.py:756
